TPU v7x, 8 devices: a whole 2x2x1 slice. The times are simulated.
8 devices in a mesh: data: 1 (over z), model: 2 (over y), stage: 4 (over x, core).
Axes of the slice: x: 2, y: 2, z: 1, core: 2. Of those that a mesh axis runs over, the one named last changes fastest.
Arguments:
- inputs: bfloat16 [12, 512, 2560], P('data')
- targets: bfloat16 [12, 512, 2560], P('data')
- w_in: bfloat16 [4, 1, 2560, 10240], P('stage', None, None, 'model')
- w_out: bfloat16 [4, 1, 10240, 2560], P('stage', None, 'model')
Outputs:
- output 1: float32 [4, 1, 2560, 10240], P(('data', 'stage'), None, None, 'model')
- output 2: float32 [4, 1, 10240, 2560], P(('data', 'stage'), None, 'model')
- output 3: float32 [1], P('data')
All inputs are finite; a program needn't handle non-finite values.
Results may differ from a plain program's by a relative error of at most 0.00358275.
Values are sent between devices in bfloat16 or wider.
A program may use at most 1 GiB of HBM per device.

v0:
```python
import jax
import jax.numpy as jnp
from jax import lax
from jax.sharding import PartitionSpec as P

GELU_COEF = 0.7978845608028654
CUBIC_COEF = 0.044715


def gelu_tanh(values):
    inner_arg = GELU_COEF * (values + CUBIC_COEF * values * values * values)
    return 0.5 * values * (1.0 + jnp.tanh(inner_arg))


def gelu_slope(values):
    tanh_val = jnp.tanh(GELU_COEF * (values + CUBIC_COEF * values * values * values))
    return 0.5 * (1.0 + tanh_val) + 0.5 * values * (1.0 - tanh_val * tanh_val) * GELU_COEF * (1.0 + 3.0 * CUBIC_COEF * values * values)


def solution(mesh):
    n_stage = mesh.shape["stage"]
    down_perm = [(src_pos, src_pos + 1) for src_pos in range(n_stage - 1)]
    up_perm = [(src_pos + 1, src_pos) for src_pos in range(n_stage - 1)]

    def stage_step(inputs, targets, w_in, w_out):
        num_micro, num_tokens, model_dim = inputs.shape
        layers_here = w_in.shape[1]
        w_in_loc = w_in[0]
        w_out_loc = w_out[0]
        stage_pos = lax.axis_index("stage")
        is_last = stage_pos == n_stage - 1
        num_ticks = num_micro + n_stage - 1
        grad_scale = 1.0 / (num_micro * num_tokens * model_dim)

        def fwd_tick(state_in, tick_num):
            recv_act, loss_sum = state_in
            mb_index = tick_num - stage_pos
            first_in = lax.dynamic_index_in_dim(inputs, jnp.clip(tick_num, 0, num_micro - 1), 0, keepdims=False)
            hidden = jnp.where(stage_pos == 0, first_in, recv_act)
            saved_in = []
            saved_pre = []
            saved_act = []
            for layer_pos in range(layers_here):
                pre_act = jnp.dot(hidden, w_in_loc[layer_pos], preferred_element_type=jnp.float32).astype(jnp.bfloat16)
                act_out = gelu_tanh(pre_act.astype(jnp.float32)).astype(jnp.bfloat16)
                part_sum = jnp.dot(act_out, w_out_loc[layer_pos], preferred_element_type=jnp.float32)
                saved_in.append(hidden)
                saved_pre.append(pre_act)
                saved_act.append(act_out)
                hidden = (hidden.astype(jnp.float32) + lax.psum(part_sum, "model")).astype(jnp.bfloat16)
            tgt_mb = lax.dynamic_index_in_dim(targets, jnp.clip(mb_index, 0, num_micro - 1), 0, keepdims=False)
            out_err = hidden.astype(jnp.float32) - tgt_mb.astype(jnp.float32)
            start_grad = (out_err * grad_scale).astype(jnp.bfloat16)
            keep_loss = is_last & (mb_index >= 0) & (mb_index < num_micro)
            loss_sum = loss_sum + jnp.where(keep_loss, 0.5 * jnp.sum(out_err * out_err), 0.0)
            sent_act = lax.ppermute(hidden, "stage", down_perm)
            return (sent_act, loss_sum), (jnp.stack(saved_in), jnp.stack(saved_pre), jnp.stack(saved_act), start_grad)

        fwd_init = (jnp.zeros((num_tokens, model_dim), jnp.bfloat16), jnp.zeros((), jnp.float32))
        (last_act, loss_sum), (all_in, all_pre, all_act, all_start) = lax.scan(fwd_tick, fwd_init, jnp.arange(num_ticks))

        def bwd_tick(state_in, tick_num):
            recv_grad, acc_in, acc_out = state_in
            mb_index = tick_num - (n_stage - 1 - stage_pos)
            is_valid = (mb_index >= 0) & (mb_index < num_micro)
            save_pos = jnp.clip(mb_index + stage_pos, 0, num_ticks - 1)
            start_here = lax.dynamic_index_in_dim(all_start, save_pos, 0, keepdims=False)
            grad_h = jnp.where(is_last, start_here, recv_grad)
            grad_h = jnp.where(is_valid, grad_h, jnp.zeros_like(grad_h))
            layer_in = lax.dynamic_index_in_dim(all_in, save_pos, 0, keepdims=False)
            layer_pre = lax.dynamic_index_in_dim(all_pre, save_pos, 0, keepdims=False)
            layer_act = lax.dynamic_index_in_dim(all_act, save_pos, 0, keepdims=False)
            new_in = list(acc_in)
            new_out = list(acc_out)
            for layer_pos in reversed(range(layers_here)):
                grad_act = jnp.einsum("bd,fd->bf", grad_h, w_out_loc[layer_pos], preferred_element_type=jnp.float32).astype(jnp.bfloat16)
                grad_pre = (gelu_slope(layer_pre[layer_pos].astype(jnp.float32)) * grad_act.astype(jnp.float32)).astype(jnp.bfloat16)
                new_out[layer_pos] = new_out[layer_pos] + jnp.einsum("bf,bd->fd", layer_act[layer_pos], grad_h, preferred_element_type=jnp.float32)
                new_in[layer_pos] = new_in[layer_pos] + jnp.einsum("bd,bf->df", layer_in[layer_pos], grad_pre, preferred_element_type=jnp.float32)
                part_sum = jnp.einsum("bf,df->bd", grad_pre, w_in_loc[layer_pos], preferred_element_type=jnp.float32)
                grad_h = (grad_h.astype(jnp.float32) + lax.psum(part_sum, "model")).astype(jnp.bfloat16)
            sent_grad = lax.ppermute(grad_h, "stage", up_perm)
            return (sent_grad, tuple(new_in), tuple(new_out)), None

        zeros_in = tuple(jnp.zeros(w_in_loc.shape[1:], jnp.float32) for layer_pos in range(layers_here))
        zeros_out = tuple(jnp.zeros(w_out_loc.shape[1:], jnp.float32) for layer_pos in range(layers_here))
        bwd_init = (jnp.zeros((num_tokens, model_dim), jnp.bfloat16), zeros_in, zeros_out)
        (first_grad, acc_in, acc_out), unused_ys = lax.scan(bwd_tick, bwd_init, jnp.arange(num_ticks))
        loss_out = jnp.reshape(lax.psum(loss_sum, "stage") * grad_scale, (1,))
        return jnp.stack(acc_in)[None], jnp.stack(acc_out)[None], loss_out

    return jax.shard_map(
        stage_step,
        mesh=mesh,
        in_specs=(P("data", None, None), P("data", None, None), P("stage", None, None, "model"), P("stage", None, "model", None)),
        out_specs=(P(("data", "stage"), None, None, "model"), P(("data", "stage"), None, "model", None), P("data")),
        check_vma=False,
    )
```

profile of v0, /device:TPU:0, one launch (start us, length us, event | category | flops | bytes accessed | tf_op | source)
XLA Modules:
  0.0 6650.9 jit_solution(6629930320248595084)
XLA Ops:
  8.8 3292.0 %while.37 = (s32[]{:T(128)}, bf16[512,2560]{1,0:T(8,128)(2,1)}, f32[]{:T(128)}, bf16[15,1,512,2560]{3,2,1,0:T(8,128)(2,1)}, bf16[15,1,512,5120]{3,2,1,0:T(8,128)...) while((s32[]{:T(128)}, bf16[512,2560]{1,0:T(8,128)(2,1)}, ...), condition=%wide.region_3.4_spmd, body=%wide.region_0.3_spmd.sunk | while | flops 26918256640 | bytes 165153232 | solution.py:60
  65.0 127.9 %all-reduce.3.cloned.1.call-done = f32[512,2560]{1,0:T(8,128)} async-done(((f32[512,2560]{1,0:T(8,128)}), f32[512,2560]{1,0:T(8,128)}) %all-reduce.3.cloned.1.call-update) | async-done | bytes 5242896 | tf_op jit(solution)/shard_map/while/body/eval_jaxpr/psum | solution.py:50
  263.3 150.7 %all-reduce.3.cloned.1.call-done = f32[512,2560]{1,0:T(8,128)} async-done(((f32[512,2560]{1,0:T(8,128)}), f32[512,2560]{1,0:T(8,128)}) %all-reduce.3.cloned.1.call-update) | async-done | bytes 5242896 | tf_op jit(solution)/shard_map/while/body/eval_jaxpr/psum | solution.py:50
  484.4 150.7 %all-reduce.3.cloned.1.call-done = f32[512,2560]{1,0:T(8,128)} async-done(((f32[512,2560]{1,0:T(8,128)}), f32[512,2560]{1,0:T(8,128)}) %all-reduce.3.cloned.1.call-update) | async-done | bytes 5242896 | tf_op jit(solution)/shard_map/while/body/eval_jaxpr/psum | solution.py:50
  705.3 150.7 %all-reduce.3.cloned.1.call-done = f32[512,2560]{1,0:T(8,128)} async-done(((f32[512,2560]{1,0:T(8,128)}), f32[512,2560]{1,0:T(8,128)}) %all-reduce.3.cloned.1.call-update) | async-done | bytes 5242896 | tf_op jit(solution)/shard_map/while/body/eval_jaxpr/psum | solution.py:50
  926.3 150.7 %all-reduce.3.cloned.1.call-done = f32[512,2560]{1,0:T(8,128)} async-done(((f32[512,2560]{1,0:T(8,128)}), f32[512,2560]{1,0:T(8,128)}) %all-reduce.3.cloned.1.call-update) | async-done | bytes 5242896 | tf_op jit(solution)/shard_map/while/body/eval_jaxpr/psum | solution.py:50
  1147.2 150.7 %all-reduce.3.cloned.1.call-done = f32[512,2560]{1,0:T(8,128)} async-done(((f32[512,2560]{1,0:T(8,128)}), f32[512,2560]{1,0:T(8,128)}) %all-reduce.3.cloned.1.call-update) | async-done | bytes 5242896 | tf_op jit(solution)/shard_map/while/body/eval_jaxpr/psum | solution.py:50
  1368.1 150.7 %all-reduce.3.cloned.1.call-done = f32[512,2560]{1,0:T(8,128)} async-done(((f32[512,2560]{1,0:T(8,128)}), f32[512,2560]{1,0:T(8,128)}) %all-reduce.3.cloned.1.call-update) | async-done | bytes 5242896 | tf_op jit(solution)/shard_map/while/body/eval_jaxpr/psum | solution.py:50
  1589.3 150.7 %all-reduce.3.cloned.1.call-done = f32[512,2560]{1,0:T(8,128)} async-done(((f32[512,2560]{1,0:T(8,128)}), f32[512,2560]{1,0:T(8,128)}) %all-reduce.3.cloned.1.call-update) | async-done | bytes 5242896 | tf_op jit(solution)/shard_map/while/body/eval_jaxpr/psum | solution.py:50
  1810.2 150.7 %all-reduce.3.cloned.1.call-done = f32[512,2560]{1,0:T(8,128)} async-done(((f32[512,2560]{1,0:T(8,128)}), f32[512,2560]{1,0:T(8,128)}) %all-reduce.3.cloned.1.call-update) | async-done | bytes 5242896 | tf_op jit(solution)/shard_map/while/body/eval_jaxpr/psum | solution.py:50
  2031.2 150.7 %all-reduce.3.cloned.1.call-done = f32[512,2560]{1,0:T(8,128)} async-done(((f32[512,2560]{1,0:T(8,128)}), f32[512,2560]{1,0:T(8,128)}) %all-reduce.3.cloned.1.call-update) | async-done | bytes 5242896 | tf_op jit(solution)/shard_map/while/body/eval_jaxpr/psum | solution.py:50
  2252.1 150.7 %all-reduce.3.cloned.1.call-done = f32[512,2560]{1,0:T(8,128)} async-done(((f32[512,2560]{1,0:T(8,128)}), f32[512,2560]{1,0:T(8,128)}) %all-reduce.3.cloned.1.call-update) | async-done | bytes 5242896 | tf_op jit(solution)/shard_map/while/body/eval_jaxpr/psum | solution.py:50
  2473.0 150.7 %all-reduce.3.cloned.1.call-done = f32[512,2560]{1,0:T(8,128)} async-done(((f32[512,2560]{1,0:T(8,128)}), f32[512,2560]{1,0:T(8,128)}) %all-reduce.3.cloned.1.call-update) | async-done | bytes 5242896 | tf_op jit(solution)/shard_map/while/body/eval_jaxpr/psum | solution.py:50
  2694.0 150.7 %all-reduce.3.cloned.1.call-done = f32[512,2560]{1,0:T(8,128)} async-done(((f32[512,2560]{1,0:T(8,128)}), f32[512,2560]{1,0:T(8,128)}) %all-reduce.3.cloned.1.call-update) | async-done | bytes 5242896 | tf_op jit(solution)/shard_map/while/body/eval_jaxpr/psum | solution.py:50
  2915.0 150.7 %all-reduce.3.cloned.1.call-done = f32[512,2560]{1,0:T(8,128)} async-done(((f32[512,2560]{1,0:T(8,128)}), f32[512,2560]{1,0:T(8,128)}) %all-reduce.3.cloned.1.call-update) | async-done | bytes 5242896 | tf_op jit(solution)/shard_map/while/body/eval_jaxpr/psum | solution.py:50
  3135.9 150.7 %all-reduce.3.cloned.1.call-done = f32[512,2560]{1,0:T(8,128)} async-done(((f32[512,2560]{1,0:T(8,128)}), f32[512,2560]{1,0:T(8,128)}) %all-reduce.3.cloned.1.call-update) | async-done | bytes 5242896 | tf_op jit(solution)/shard_map/while/body/eval_jaxpr/psum | solution.py:50
  3303.0 3330.2 %while.38 = (s32[]{:T(128)}, bf16[512,2560]{1,0:T(8,128)(2,1)}, f32[2560,5120]{1,0:T(8,128)}, f32[5120,2560]{1,0:T(8,128)}, s32[15]{0:T(128)}, /*index=5*/s32[]{...) while((s32[]{:T(128)}, bf16[512,2560]{1,0:T(8,128)(2,1)}, ...), condition=%wide.region_6.7_spmd.clone, body=%wide.region_4.6_spmd.clone.sunk | while | flops 53805056000 | bytes 372244864 | solution.py:88
  3377.4 126.6 %all-reduce.5.cloned.1.call-done = f32[512,2560]{1,0:T(8,128)} async-done(((f32[512,2560]{1,0:T(8,128)}), f32[512,2560]{1,0:T(8,128)}) %all-reduce.5.cloned.1.call-update) | async-done | bytes 5242896 | tf_op jit(solution)/shard_map/while/body/eval_jaxpr/psum | solution.py:81
  3627.5 89.8 %all-reduce.5.cloned.1.call-done = f32[512,2560]{1,0:T(8,128)} async-done(((f32[512,2560]{1,0:T(8,128)}), f32[512,2560]{1,0:T(8,128)}) %all-reduce.5.cloned.1.call-update) | async-done | bytes 5242896 | tf_op jit(solution)/shard_map/while/body/eval_jaxpr/psum | solution.py:81
  3853.8 84.5 %all-reduce.5.cloned.1.call-done = f32[512,2560]{1,0:T(8,128)} async-done(((f32[512,2560]{1,0:T(8,128)}), f32[512,2560]{1,0:T(8,128)}) %all-reduce.5.cloned.1.call-update) | async-done | bytes 5242896 | tf_op jit(solution)/shard_map/while/body/eval_jaxpr/psum | solution.py:81
  4074.7 84.4 %all-reduce.5.cloned.1.call-done = f32[512,2560]{1,0:T(8,128)} async-done(((f32[512,2560]{1,0:T(8,128)}), f32[512,2560]{1,0:T(8,128)}) %all-reduce.5.cloned.1.call-update) | async-done | bytes 5242896 | tf_op jit(solution)/shard_map/while/body/eval_jaxpr/psum | solution.py:81
  4295.5 84.4 %all-reduce.5.cloned.1.call-done = f32[512,2560]{1,0:T(8,128)} async-done(((f32[512,2560]{1,0:T(8,128)}), f32[512,2560]{1,0:T(8,128)}) %all-reduce.5.cloned.1.call-update) | async-done | bytes 5242896 | tf_op jit(solution)/shard_map/while/body/eval_jaxpr/psum | solution.py:81
  4516.4 84.4 %all-reduce.5.cloned.1.call-done = f32[512,2560]{1,0:T(8,128)} async-done(((f32[512,2560]{1,0:T(8,128)}), f32[512,2560]{1,0:T(8,128)}) %all-reduce.5.cloned.1.call-update) | async-done | bytes 5242896 | tf_op jit(solution)/shard_map/while/body/eval_jaxpr/psum | solution.py:81
  4737.2 84.4 %all-reduce.5.cloned.1.call-done = f32[512,2560]{1,0:T(8,128)} async-done(((f32[512,2560]{1,0:T(8,128)}), f32[512,2560]{1,0:T(8,128)}) %all-reduce.5.cloned.1.call-update) | async-done | bytes 5242896 | tf_op jit(solution)/shard_map/while/body/eval_jaxpr/psum | solution.py:81
  4958.0 84.4 %all-reduce.5.cloned.1.call-done = f32[512,2560]{1,0:T(8,128)} async-done(((f32[512,2560]{1,0:T(8,128)}), f32[512,2560]{1,0:T(8,128)}) %all-reduce.5.cloned.1.call-update) | async-done | bytes 5242896 | tf_op jit(solution)/shard_map/while/body/eval_jaxpr/psum | solution.py:81
  5178.8 84.5 %all-reduce.5.cloned.1.call-done = f32[512,2560]{1,0:T(8,128)} async-done(((f32[512,2560]{1,0:T(8,128)}), f32[512,2560]{1,0:T(8,128)}) %all-reduce.5.cloned.1.call-update) | async-done | bytes 5242896 | tf_op jit(solution)/shard_map/while/body/eval_jaxpr/psum | solution.py:81
  5399.7 84.5 %all-reduce.5.cloned.1.call-done = f32[512,2560]{1,0:T(8,128)} async-done(((f32[512,2560]{1,0:T(8,128)}), f32[512,2560]{1,0:T(8,128)}) %all-reduce.5.cloned.1.call-update) | async-done | bytes 5242896 | tf_op jit(solution)/shard_map/while/body/eval_jaxpr/psum | solution.py:81
  5620.7 84.4 %all-reduce.5.cloned.1.call-done = f32[512,2560]{1,0:T(8,128)} async-done(((f32[512,2560]{1,0:T(8,128)}), f32[512,2560]{1,0:T(8,128)}) %all-reduce.5.cloned.1.call-update) | async-done | bytes 5242896 | tf_op jit(solution)/shard_map/while/body/eval_jaxpr/psum | solution.py:81
  5841.6 84.5 %all-reduce.5.cloned.1.call-done = f32[512,2560]{1,0:T(8,128)} async-done(((f32[512,2560]{1,0:T(8,128)}), f32[512,2560]{1,0:T(8,128)}) %all-reduce.5.cloned.1.call-update) | async-done | bytes 5242896 | tf_op jit(solution)/shard_map/while/body/eval_jaxpr/psum | solution.py:81
  6062.5 84.4 %all-reduce.5.cloned.1.call-done = f32[512,2560]{1,0:T(8,128)} async-done(((f32[512,2560]{1,0:T(8,128)}), f32[512,2560]{1,0:T(8,128)}) %all-reduce.5.cloned.1.call-update) | async-done | bytes 5242896 | tf_op jit(solution)/shard_map/while/body/eval_jaxpr/psum | solution.py:81
  6283.4 84.3 %all-reduce.5.cloned.1.call-done = f32[512,2560]{1,0:T(8,128)} async-done(((f32[512,2560]{1,0:T(8,128)}), f32[512,2560]{1,0:T(8,128)}) %all-reduce.5.cloned.1.call-update) | async-done | bytes 5242896 | tf_op jit(solution)/shard_map/while/body/eval_jaxpr/psum | solution.py:81
  6504.1 84.4 %all-reduce.5.cloned.1.call-done = f32[512,2560]{1,0:T(8,128)} async-done(((f32[512,2560]{1,0:T(8,128)}), f32[512,2560]{1,0:T(8,128)}) %all-reduce.5.cloned.1.call-update) | async-done | bytes 5242896 | tf_op jit(solution)/shard_map/while/body/eval_jaxpr/psum | solution.py:81
  (386 shorter events, 3044.6 us)
Async XLA Ops:
  8.9 184.1 %all-reduce.3.cloned.1.call-start = ((), (), s32[]{:S(2)}) async-start(), calls=%async_computation | async-start | bytes 10485760 | tf_op jit(solution)/shard_map/while/body/eval_jaxpr/psum | solution.py:50
  207.0 207.0 %all-reduce.3.cloned.1.call-start = ((), (), s32[]{:S(2)}) async-start(), calls=%async_computation | async-start | bytes 10485760 | tf_op jit(solution)/shard_map/while/body/eval_jaxpr/psum | solution.py:50
  428.0 207.0 %all-reduce.3.cloned.1.call-start = ((), (), s32[]{:S(2)}) async-start(), calls=%async_computation | async-start | bytes 10485760 | tf_op jit(solution)/shard_map/while/body/eval_jaxpr/psum | solution.py:50
  649.2 206.8 %all-reduce.3.cloned.1.call-start = ((), (), s32[]{:S(2)}) async-start(), calls=%async_computation | async-start | bytes 10485760 | tf_op jit(solution)/shard_map/while/body/eval_jaxpr/psum | solution.py:50
  870.1 206.8 %all-reduce.3.cloned.1.call-start = ((), (), s32[]{:S(2)}) async-start(), calls=%async_computation | async-start | bytes 10485760 | tf_op jit(solution)/shard_map/while/body/eval_jaxpr/psum | solution.py:50
  1091.0 206.9 %all-reduce.3.cloned.1.call-start = ((), (), s32[]{:S(2)}) async-start(), calls=%async_computation | async-start | bytes 10485760 | tf_op jit(solution)/shard_map/while/body/eval_jaxpr/psum | solution.py:50
  1312.0 206.9 %all-reduce.3.cloned.1.call-start = ((), (), s32[]{:S(2)}) async-start(), calls=%async_computation | async-start | bytes 10485760 | tf_op jit(solution)/shard_map/while/body/eval_jaxpr/psum | solution.py:50
  1533.1 206.9 %all-reduce.3.cloned.1.call-start = ((), (), s32[]{:S(2)}) async-start(), calls=%async_computation | async-start | bytes 10485760 | tf_op jit(solution)/shard_map/while/body/eval_jaxpr/psum | solution.py:50
  1754.1 206.9 %all-reduce.3.cloned.1.call-start = ((), (), s32[]{:S(2)}) async-start(), calls=%async_computation | async-start | bytes 10485760 | tf_op jit(solution)/shard_map/while/body/eval_jaxpr/psum | solution.py:50
  1975.0 206.9 %all-reduce.3.cloned.1.call-start = ((), (), s32[]{:S(2)}) async-start(), calls=%async_computation | async-start | bytes 10485760 | tf_op jit(solution)/shard_map/while/body/eval_jaxpr/psum | solution.py:50
  2196.0 206.8 %all-reduce.3.cloned.1.call-start = ((), (), s32[]{:S(2)}) async-start(), calls=%async_computation | async-start | bytes 10485760 | tf_op jit(solution)/shard_map/while/body/eval_jaxpr/psum | solution.py:50
  2416.9 206.8 %all-reduce.3.cloned.1.call-start = ((), (), s32[]{:S(2)}) async-start(), calls=%async_computation | async-start | bytes 10485760 | tf_op jit(solution)/shard_map/while/body/eval_jaxpr/psum | solution.py:50
  2637.8 206.9 %all-reduce.3.cloned.1.call-start = ((), (), s32[]{:S(2)}) async-start(), calls=%async_computation | async-start | bytes 10485760 | tf_op jit(solution)/shard_map/while/body/eval_jaxpr/psum | solution.py:50
  2858.8 206.9 %all-reduce.3.cloned.1.call-start = ((), (), s32[]{:S(2)}) async-start(), calls=%async_computation | async-start | bytes 10485760 | tf_op jit(solution)/shard_map/while/body/eval_jaxpr/psum | solution.py:50
  3079.8 206.8 %all-reduce.3.cloned.1.call-start = ((), (), s32[]{:S(2)}) async-start(), calls=%async_computation | async-start | bytes 10485760 | tf_op jit(solution)/shard_map/while/body/eval_jaxpr/psum | solution.py:50
  3303.0 201.0 %all-reduce.5.cloned.1.call-start = ((), (), s32[]{:S(2)}) async-start(), calls=%async_computation.1 | async-start | bytes 10485760 | tf_op jit(solution)/shard_map/while/body/eval_jaxpr/psum | solution.py:81
  3535.7 181.6 %all-reduce.5.cloned.1.call-start = ((), (), s32[]{:S(2)}) async-start(), calls=%async_computation.1 | async-start | bytes 10485760 | tf_op jit(solution)/shard_map/while/body/eval_jaxpr/psum | solution.py:81
  3762.0 176.3 %all-reduce.5.cloned.1.call-start = ((), (), s32[]{:S(2)}) async-start(), calls=%async_computation.1 | async-start | bytes 10485760 | tf_op jit(solution)/shard_map/while/body/eval_jaxpr/psum | solution.py:81
  3982.9 176.2 %all-reduce.5.cloned.1.call-start = ((), (), s32[]{:S(2)}) async-start(), calls=%async_computation.1 | async-start | bytes 10485760 | tf_op jit(solution)/shard_map/while/body/eval_jaxpr/psum | solution.py:81
  4203.7 176.2 %all-reduce.5.cloned.1.call-start = ((), (), s32[]{:S(2)}) async-start(), calls=%async_computation.1 | async-start | bytes 10485760 | tf_op jit(solution)/shard_map/while/body/eval_jaxpr/psum | solution.py:81
  4424.5 176.2 %all-reduce.5.cloned.1.call-start = ((), (), s32[]{:S(2)}) async-start(), calls=%async_computation.1 | async-start | bytes 10485760 | tf_op jit(solution)/shard_map/while/body/eval_jaxpr/psum | solution.py:81
  4605.5 38.5 collective-permute-start.1
  4645.5 176.2 %all-reduce.5.cloned.1.call-start = ((), (), s32[]{:S(2)}) async-start(), calls=%async_computation.1 | async-start | bytes 10485760 | tf_op jit(solution)/shard_map/while/body/eval_jaxpr/psum | solution.py:81
  4866.3 176.2 %all-reduce.5.cloned.1.call-start = ((), (), s32[]{:S(2)}) async-start(), calls=%async_computation.1 | async-start | bytes 10485760 | tf_op jit(solution)/shard_map/while/body/eval_jaxpr/psum | solution.py:81
  5087.1 176.3 %all-reduce.5.cloned.1.call-start = ((), (), s32[]{:S(2)}) async-start(), calls=%async_computation.1 | async-start | bytes 10485760 | tf_op jit(solution)/shard_map/while/body/eval_jaxpr/psum | solution.py:81
  5308.0 176.3 %all-reduce.5.cloned.1.call-start = ((), (), s32[]{:S(2)}) async-start(), calls=%async_computation.1 | async-start | bytes 10485760 | tf_op jit(solution)/shard_map/while/body/eval_jaxpr/psum | solution.py:81
  5489.0 38.5 collective-permute-start.1
  5529.0 176.2 %all-reduce.5.cloned.1.call-start = ((), (), s32[]{:S(2)}) async-start(), calls=%async_computation.1 | async-start | bytes 10485760 | tf_op jit(solution)/shard_map/while/body/eval_jaxpr/psum | solution.py:81
  5749.8 176.2 %all-reduce.5.cloned.1.call-start = ((), (), s32[]{:S(2)}) async-start(), calls=%async_computation.1 | async-start | bytes 10485760 | tf_op jit(solution)/shard_map/while/body/eval_jaxpr/psum | solution.py:81
  5970.7 176.1 %all-reduce.5.cloned.1.call-start = ((), (), s32[]{:S(2)}) async-start(), calls=%async_computation.1 | async-start | bytes 10485760 | tf_op jit(solution)/shard_map/while/body/eval_jaxpr/psum | solution.py:81
  6191.6 176.1 %all-reduce.5.cloned.1.call-start = ((), (), s32[]{:S(2)}) async-start(), calls=%async_computation.1 | async-start | bytes 10485760 | tf_op jit(solution)/shard_map/while/body/eval_jaxpr/psum | solution.py:81
  6412.4 176.1 %all-reduce.5.cloned.1.call-start = ((), (), s32[]{:S(2)}) async-start(), calls=%async_computation.1 | async-start | bytes 10485760 | tf_op jit(solution)/shard_map/while/body/eval_jaxpr/psum | solution.py:81
  (58 other events, 984.9 us)
Sparse Core Ops, SparseCore 0:
  64.6 128.2 all-reduce.2
  262.8 151.1 all-reduce.2
  484.0 151.0 all-reduce.2
  704.8 151.1 all-reduce.2
  925.8 151.0 all-reduce.2
  1146.8 151.0 all-reduce.2
  1367.7 151.1 all-reduce.2
  1588.9 151.0 all-reduce.2
  1809.8 151.1 all-reduce.2
  2030.8 151.0 all-reduce.2
  2251.7 151.0 all-reduce.2
  2472.6 151.1 all-reduce.2
  2693.5 151.1 all-reduce.2
  2914.5 151.0 all-reduce.2
  3135.5 151.0 all-reduce.2
  3353.8 150.1 all-reduce.4
  3586.6 130.7 all-reduce.4
  3812.8 125.3 all-reduce.4
  4033.7 125.2 all-reduce.4
  4254.6 125.2 all-reduce.4
  4475.3 125.3 all-reduce.4
  4696.3 125.3 all-reduce.4
  4917.1 125.3 all-reduce.4
  5137.9 125.4 all-reduce.4
  5358.8 125.4 all-reduce.4
  5579.8 125.3 all-reduce.4
  5800.6 125.3 all-reduce.4
  6021.6 125.2 all-reduce.4
  6242.4 125.2 all-reduce.4
  6463.2 125.2 all-reduce.4
where the time goes:
time: 6660 us; the launch traced here: 6650 us
  waiting for transfers between devices  3550 us (53%)
  matrix products  2590 us (39%)
  other arithmetic  329 us (5%)
    psum x15, waiting for transfers between devices, fwd_tick(): lax.psum(part_sum, 'model')  2240 us
    psum x15, waiting for transfers between devices, bwd_tick(): lax.psum(part_sum, 'model')  1310 us
    dot_general x15, matrix products, bwd_tick(): jnp.einsum('bf,bd->fd', layer_act[layer_pos], grad_h, preferred_element_t...  599 us
    dot_general x15, matrix products, bwd_tick(): jnp.einsum('bd,bf->df', layer_in[layer_pos], grad_pre, preferred_element_...  544 us
    dot_general x15, matrix products, fwd_tick(): jnp.dot(act_out, w_out_loc[layer_pos], preferred_element_type=jnp.float32)  390 us
    dot_general x15, matrix products, bwd_tick(): jnp.einsum('bd,fd->bf', grad_h, w_out_loc[layer_pos], preferred_element_t...  370 us
    dot_general x15, matrix products, fwd_tick(): jnp.dot(hidden, w_in_loc[layer_pos], preferred_element_type=jnp.float32)  367 us
    dot_general x15, matrix products, bwd_tick(): jnp.einsum('bf,df->bd', grad_pre, w_in_loc[layer_pos], preferred_element_...  319 us
  transfers between devices with their start and end apart: 60, of which 30 were waited for; matrix products, arithmetic and copies ran while one was open for 18% of the time, Pallas kernels for 0%

commit v1 on v0

v1 whole, which is shorter than its diff:
```python
import jax
import jax.numpy as jnp
from jax import lax
from jax.experimental import pallas as pl
from jax.experimental.pallas import tpu as pltpu
from jax.sharding import PartitionSpec as P

GELU_COEF = 0.7978845608028654
CUBIC_COEF = 0.044715

N_MB = 24
TOK = 256
HALF = TOK // 2
DIM = 2560
HID = 5120
HB = 512
N_BLK = HID // HB
GROUP = 4
N_GRP = N_MB // GROUP - 1
GTOK = GROUP * TOK
N_ELEM = N_MB * TOK * DIM
MESH = pl.DeviceIdType.MESH
BF = jnp.bfloat16
F32 = jnp.float32


def dot_nn(a, b):
    return lax.dot_general(a, b, (((1,), (0,)), ((), ())), preferred_element_type=F32)


def dot_nt(a, b):
    return lax.dot_general(a, b, (((1,), (1,)), ((), ())), preferred_element_type=F32)


def dot_tn(a, b):
    return lax.dot_general(a, b, (((0,), (0,)), ((), ())), preferred_element_type=F32)


def gelu(v):
    return 0.5 * v * (1.0 + jnp.tanh(GELU_COEF * (v + CUBIC_COEF * v * v * v)))


def gelu_slope(v):
    t = jnp.tanh(GELU_COEF * (v + CUBIC_COEF * v * v * v))
    return 0.5 * (1.0 + t) + 0.5 * v * (1.0 - t * t) * GELU_COEF * (1.0 + 3.0 * CUBIC_COEF * v * v)


def pipeline_kernel(
    x_in, tgt, w1, w2,
    x_all, e_all, u_all, a_all, g_all, rsf, rsb, acc1, acc2, loss,
    xbuf, w1buf, w2buf, ubuf, abuf, gbuf, uin, accf, accb, rsv, res, tbuf, yf, yb, wide, narrow, wtile,
    w_sem, x_sem, uo_sem, ao_sem, go_sem, ui_sem, p_sem, wd_sem, wn_sem, wl_sem, ws_sem,
    xr_sem, er_sem, rf_sem, rb_sem, sf_sem, sb_sem, yf_sem, yb_sem,
):
    my = lax.axis_index("model")
    st = lax.axis_index("stage")
    other = 1 - my
    last = st == 3
    first = st == 0
    warm = jnp.where(st == 0, 16, jnp.where(st == 1, 12, jnp.where(st == 2, 6, 2)))
    partner = {"model": other}
    nxt = jnp.minimum(st + 1, 3)
    prv = jnp.maximum(st - 1, 0)

    def rows_of(m, half):
        return pl.ds(pl.multiple_of(m * TOK + half * HALF, HALF), HALF)

    def mb_rows(m):
        return pl.ds(pl.multiple_of(m * TOK, TOK), TOK)

    def half_rows(half):
        return pl.ds(pl.multiple_of(half * HALF, HALF), HALF)

    def cols(j, width=HB):
        return pl.ds(pl.multiple_of(j * width, width), width)

    def w_copies(j, slot):
        return (
            pltpu.make_async_copy(w1.at[:, cols(j)], w1buf.at[slot], w_sem.at[slot, 0]),
            pltpu.make_async_copy(w2.at[cols(j), :], w2buf.at[slot], w_sem.at[slot, 1]),
        )

    def rs_copy(acc, slot, buf, m, send, recv):
        return pltpu.make_async_remote_copy(
            src_ref=acc.at[slot, half_rows(other), :],
            dst_ref=buf.at[pl.ds(pl.multiple_of(m * HALF, HALF), HALF), :],
            send_sem=send.at[slot],
            recv_sem=recv.at[m],
            device_id=partner,
            device_id_type=MESH,
        )

    def half_copy(src, slot, dst, m, half, send, k, recv, dev):
        return pltpu.make_async_remote_copy(
            src_ref=src.at[slot],
            dst_ref=dst.at[rows_of(m, half), :],
            send_sem=send.at[slot, k],
            recv_sem=recv.at[m, half],
            device_id=dev,
            device_id_type=MESH,
        )

    def yf_pair(m, slot):
        return (
            half_copy(yf, slot, x_all, m, my, yf_sem, 0, xr_sem, {"model": my, "stage": nxt}),
            half_copy(yf, slot, x_all, m, my, yf_sem, 1, xr_sem, {"model": other, "stage": nxt}),
        )

    def yl_own(m, slot):
        return pltpu.make_async_copy(yf.at[slot], e_all.at[rows_of(m, my), :], er_sem.at[m, my])

    def yl_send(m, slot):
        return half_copy(yf, slot, e_all, m, my, yf_sem, 1, er_sem, partner)

    def yb_pair(m, slot):
        return (
            half_copy(yb, slot, e_all, m, my, yb_sem, 0, er_sem, {"model": my, "stage": prv}),
            half_copy(yb, slot, e_all, m, my, yb_sem, 1, er_sem, {"model": other, "stage": prv}),
        )

    def wait_in(dst, m, recv):
        for half in range(2):
            ref = dst.at[rows_of(m, half), :]
            pltpu.make_async_copy(ref, ref, recv.at[m, half]).wait()

    def out_copy(buf, slot, dst, m, j, sem):
        return pltpu.make_async_copy(buf.at[slot], dst.at[mb_rows(m), cols(j)], sem.at[slot])

    def u_load(m, j, slot):
        return pltpu.make_async_copy(u_all.at[mb_rows(m), cols(j)], uin.at[slot], ui_sem.at[slot])

    def load_x(src, m):
        cp = pltpu.make_async_copy(src.at[mb_rows(m), :], xbuf, x_sem)
        cp.start()
        cp.wait()

    def forward(m):
        slot_m = lax.rem(m, 2)

        @pl.when(first)
        def _():
            load_x(x_in, m)

        @pl.when(jnp.logical_not(first))
        def _():
            wait_in(x_all, m, xr_sem)
            load_x(x_all, m)

        @pl.when(m >= 2)
        def _():
            rs_copy(accf, slot_m, rsf, m - 2, sf_sem, rf_sem).wait_send()

        @pl.loop(0, N_BLK)
        def _(j):
            slot = lax.rem(j, 2)
            for cp in w_copies(j, slot):
                cp.wait()
            for cp in w_copies(lax.rem(j + 1, N_BLK), 1 - slot):
                cp.start()

            @pl.when(m * N_BLK + j >= 2)
            def _():
                out_copy(ubuf, slot, u_all, m, j, uo_sem).wait()
                out_copy(abuf, slot, a_all, m, j, ao_sem).wait()

            ubuf[slot] = dot_nn(xbuf[...], w1buf[slot]).astype(BF)
            abuf[slot] = gelu(ubuf[slot].astype(F32)).astype(BF)
            out_copy(ubuf, slot, u_all, m, j, uo_sem).start()
            out_copy(abuf, slot, a_all, m, j, ao_sem).start()

            @pl.when(j == 0)
            def _():
                accf[slot_m] = jnp.zeros((TOK, DIM), F32)

            accf[slot_m] += dot_nn(abuf[slot], w2buf[slot])

        rs_copy(accf, slot_m, rsf, m, sf_sem, rf_sem).start()

        @pl.when(m == N_MB - 1)
        def _():
            for slot in range(2):
                out_copy(ubuf, slot, u_all, m, slot, uo_sem).wait()
                out_copy(abuf, slot, a_all, m, slot, ao_sem).wait()

    def load_post(acc_buf, m, recv, src):
        ref = acc_buf.at[pl.ds(pl.multiple_of(m * HALF, HALF), HALF), :]
        pltpu.make_async_copy(ref, ref, recv.at[m]).wait()
        a = pltpu.make_async_copy(ref, rsv, p_sem.at[0])
        a.start()
        b = pltpu.make_async_copy(src.at[rows_of(m, my), :], res, p_sem.at[1])
        b.start()
        return a, b

    def forward_post(m):
        slot = lax.rem(m, 2)

        def run(src):
            t = pltpu.make_async_copy(tgt.at[rows_of(m, my), :], tbuf, p_sem.at[2])
            t.start()
            for cp in load_post(rsf, m, rf_sem, src):
                cp.wait()
            t.wait()

        @pl.when(first)
        def _():
            run(x_in)

        @pl.when(jnp.logical_not(first))
        def _():
            run(x_all)

        @pl.when(m >= 2)
        def _():
            @pl.when(last)
            def _():
                yl_send(m, slot).wait_send()

            @pl.when(jnp.logical_not(last))
            def _():
                for cp in yf_pair(m, slot):
                    cp.wait_send()

        y = (res[...].astype(F32) + (accf[slot, half_rows(my), :] + rsv[...])).astype(BF)

        @pl.when(jnp.logical_not(last))
        def _():
            yf[slot] = y
            for cp in yf_pair(m, slot):
                cp.start()

        @pl.when(last)
        def _():
            err = y.astype(F32) - tbuf[...].astype(F32)
            yf[slot] = (err * (1.0 / N_ELEM)).astype(BF)
            sq = err * err
            part = sq[:, 0:128]
            for c in range(1, DIM // 128):
                part = part + sq[:, c * 128 : (c + 1) * 128]
            loss[...] += jnp.sum(part.reshape(HALF // 8, 8, 128), axis=0)
            yl_own(m, slot).start()
            yl_send(m, slot).start()

    def backward(m):
        slot_m = lax.rem(m, 2)
        u_load(m, 0, 0).start()
        wait_in(e_all, m, er_sem)
        load_x(e_all, m)

        @pl.when(jnp.logical_and(m >= 2, jnp.logical_not(first)))
        def _():
            rs_copy(accb, slot_m, rsb, m - 2, sb_sem, rb_sem).wait_send()

        @pl.loop(0, N_BLK)
        def _(j):
            slot = lax.rem(j, 2)
            for cp in w_copies(j, slot):
                cp.wait()
            for cp in w_copies(lax.rem(j + 1, N_BLK), 1 - slot):
                cp.start()
            u_load(m, j, slot).wait()

            @pl.when(j + 1 < N_BLK)
            def _():
                u_load(m, j + 1, 1 - slot).start()

            @pl.when(m * N_BLK + j >= 2)
            def _():
                out_copy(gbuf, slot, g_all, m, j, go_sem).wait()

            q = dot_nt(xbuf[...], w2buf[slot]).astype(BF)
            gbuf[slot] = (gelu_slope(uin[slot].astype(F32)) * q.astype(F32)).astype(BF)
            out_copy(gbuf, slot, g_all, m, j, go_sem).start()

            @pl.when(jnp.logical_not(first))
            def _():
                @pl.when(j == 0)
                def _():
                    accb[slot_m] = jnp.zeros((TOK, DIM), F32)

                accb[slot_m] += dot_nt(gbuf[slot], w1buf[slot])

        @pl.when(jnp.logical_not(first))
        def _():
            rs_copy(accb, slot_m, rsb, m, sb_sem, rb_sem).start()

    def backward_post(m):
        slot = lax.rem(m, 2)
        for cp in load_post(rsb, m, rb_sem, e_all):
            cp.wait()

        @pl.when(m >= 2)
        def _():
            for cp in yb_pair(m, slot):
                cp.wait_send()

        yb[slot] = (res[...].astype(F32) + (accb[slot, half_rows(my), :] + rsv[...])).astype(BF)
        for cp in yb_pair(m, slot):
            cp.start()

    def weight_step(v):
        grp = v // GROUP
        quart = lax.rem(v, GROUP)
        rows = pl.ds(pl.multiple_of(grp * GTOK, GTOK), GTOK)
        out2 = quart < 2

        def on_tile(t, fn2, fn1):
            @pl.when(out2)
            def _():
                fn2(cols(quart * 5 + t))

            @pl.when(jnp.logical_not(out2))
            def _():
                fn1(cols(t), cols(quart - 2, DIM))

        def start_narrow(t, slot):
            def fn2(blk):
                pltpu.make_async_copy(a_all.at[rows, blk], narrow.at[slot], wn_sem.at[slot]).start()

            def fn1(dblk, half):
                @pl.when(first)
                def _():
                    pltpu.make_async_copy(x_in.at[rows, dblk], narrow.at[slot], wn_sem.at[slot]).start()

                @pl.when(jnp.logical_not(first))
                def _():
                    pltpu.make_async_copy(x_all.at[rows, dblk], narrow.at[slot], wn_sem.at[slot]).start()

            on_tile(t, fn2, fn1)

        def start_tile(t, slot):
            def fn2(blk):
                pltpu.make_async_copy(acc2.at[blk, :], wtile.at[slot], wl_sem.at[slot]).start()

            def fn1(dblk, half):
                pltpu.make_async_copy(acc1.at[dblk, half], wtile.at[slot], wl_sem.at[slot]).start()

            on_tile(t, fn2, fn1)

        def start_store(t, slot):
            def fn2(blk):
                pltpu.make_async_copy(wtile.at[slot], acc2.at[blk, :], ws_sem.at[slot]).start()

            def fn1(dblk, half):
                pltpu.make_async_copy(wtile.at[slot], acc1.at[dblk, half], ws_sem.at[slot]).start()

            on_tile(t, fn2, fn1)

        def wait_store(slot):
            pltpu.make_async_copy(wtile.at[slot], acc2.at[pl.ds(0, HB), :], ws_sem.at[slot]).wait()

        @pl.when(out2)
        def _():
            pltpu.make_async_copy(e_all.at[rows, :], wide, wd_sem).start()

        @pl.when(jnp.logical_not(out2))
        def _():
            pltpu.make_async_copy(g_all.at[rows, cols(quart - 2, DIM)], wide, wd_sem).start()

        start_narrow(0, 0)

        @pl.when(grp > 0)
        def _():
            start_tile(0, 0)

        pltpu.make_async_copy(e_all.at[rows, :], wide, wd_sem).wait()

        @pl.loop(0, 5)
        def _(t):
            slot = lax.rem(t, 2)
            pltpu.make_async_copy(a_all.at[rows, pl.ds(0, HB)], narrow.at[slot], wn_sem.at[slot]).wait()

            @pl.when(grp > 0)
            def _():
                pltpu.make_async_copy(acc2.at[pl.ds(0, HB), :], wtile.at[slot], wl_sem.at[slot]).wait()

            @pl.when(t >= 1)
            def _():
                wait_store(1 - slot)

            @pl.when(t < 4)
            def _():
                start_narrow(t + 1, 1 - slot)

                @pl.when(grp > 0)
                def _():
                    start_tile(t + 1, 1 - slot)

            @pl.when(grp == 0)
            def _():
                wtile[slot] = jnp.zeros((HB, DIM), F32)

            wtile[slot] += dot_tn(narrow[slot], wide[...])
            start_store(t, slot)

        wait_store(0)

    loss[...] = jnp.zeros((8, 128), F32)
    for cp in w_copies(0, 0):
        cp.start()

    @pl.loop(0, N_MB + warm)
    def _(k):
        b = k - warm
        p = k - 1
        v = b - GROUP
        b_on = b >= 0
        f_on = k < N_MB
        p_on = jnp.logical_and(p >= 0, p < N_MB)
        pb_on = jnp.logical_and(b_on, jnp.logical_not(first))

        @pl.when(b_on)
        def _():
            backward(b)

        @pl.when(jnp.logical_and(b_on, p_on))
        def _():
            forward_post(p)

        @pl.when(f_on)
        def _():
            forward(k)

        @pl.when(jnp.logical_and(jnp.logical_not(b_on), p_on))
        def _():
            forward_post(p)

        @pl.when(jnp.logical_and(pb_on, f_on))
        def _():
            backward_post(b)

        @pl.when(v >= 0)
        def _():
            weight_step(v)

        @pl.when(jnp.logical_and(pb_on, jnp.logical_not(f_on)))
        def _():
            backward_post(b)

    for cp in w_copies(0, 0):
        cp.wait()
    for m in (N_MB - 2, N_MB - 1):
        slot = m % 2
        out_copy(gbuf, slot, g_all, m, 0, go_sem).wait()
        rs_copy(accf, slot, rsf, m, sf_sem, rf_sem).wait_send()

        @pl.when(jnp.logical_not(first))
        def _():
            rs_copy(accb, slot, rsb, m, sb_sem, rb_sem).wait_send()
            for cp in yb_pair(m, slot):
                cp.wait_send()

        @pl.when(last)
        def _():
            yl_send(m, slot).wait_send()

        @pl.when(jnp.logical_not(last))
        def _():
            for cp in yf_pair(m, slot):
                cp.wait_send()


def run_pipeline(x_in, tgt, w1, w2):
    tokens = N_MB * TOK
    hbm = pl.BlockSpec(memory_space=pl.ANY)
    dma = pltpu.SemaphoreType.DMA
    shapes = [
        ((tokens, DIM), BF), ((tokens, DIM), BF),
        ((tokens, HID), BF), ((tokens, HID), BF), ((tokens, HID), BF),
        ((tokens // 2, DIM), F32), ((tokens // 2, DIM), F32),
        ((DIM, HID), F32), ((HID, DIM), F32),
    ]
    out_shape = [jax.ShapeDtypeStruct(s, d) for s, d in shapes] + [jax.ShapeDtypeStruct((8, 128), F32)]
    return pl.pallas_call(
        pipeline_kernel,
        out_shape=out_shape,
        in_specs=[hbm] * 4,
        out_specs=[hbm] * 9 + [pl.BlockSpec(memory_space=pltpu.VMEM)],
        scratch_shapes=[
            pltpu.VMEM((TOK, DIM), BF),
            pltpu.VMEM((2, DIM, HB), BF),
            pltpu.VMEM((2, HB, DIM), BF),
            pltpu.VMEM((2, TOK, HB), BF),
            pltpu.VMEM((2, TOK, HB), BF),
            pltpu.VMEM((2, TOK, HB), BF),
            pltpu.VMEM((2, TOK, HB), BF),
            pltpu.VMEM((2, TOK, DIM), F32),
            pltpu.VMEM((2, TOK, DIM), F32),
            pltpu.VMEM((HALF, DIM), F32),
            pltpu.VMEM((HALF, DIM), BF),
            pltpu.VMEM((HALF, DIM), BF),
            pltpu.VMEM((2, HALF, DIM), BF),
            pltpu.VMEM((2, HALF, DIM), BF),
            pltpu.VMEM((GTOK, DIM), BF),
            pltpu.VMEM((2, GTOK, HB), BF),
            pltpu.VMEM((2, HB, DIM), F32),
            dma((2, 2)), dma, dma((2,)), dma((2,)), dma((2,)), dma((2,)), dma((3,)), dma, dma((2,)), dma((2,)), dma((2,)),
            dma((N_MB, 2)), dma((N_MB, 2)), dma((N_MB,)), dma((N_MB,)), dma((2,)), dma((2,)), dma((2, 2)), dma((2, 2)),
        ],
        compiler_params=pltpu.CompilerParams(vmem_limit_bytes=66_000_000, has_side_effects=True),
        name="pipeline",
    )(x_in, tgt, w1, w2)


def solution(mesh):
    def stage_step(inputs, targets, w_in, w_out):
        tokens = N_MB * TOK
        x_in = inputs.reshape(tokens, DIM)
        tgt = targets.reshape(tokens, DIM)
        x_all, e_all, _, a_all, g_all, _, _, acc1, acc2, loss = run_pipeline(x_in, tgt, w_in[0, 0], w_out[0, 0])
        tail = slice(N_GRP * GTOK, tokens)
        x_tail = jnp.where(lax.axis_index("stage") == 0, x_in[tail], x_all[tail])
        grad_in = acc1 + dot_tn(x_tail, g_all[tail])
        grad_out = acc2 + dot_tn(a_all[tail], e_all[tail])
        total = lax.psum(jnp.sum(loss), ("model", "stage")) * (0.5 / N_ELEM)
        return grad_in[None, None], grad_out[None, None], jnp.reshape(total, (1,))

    return jax.shard_map(
        stage_step,
        mesh=mesh,
        in_specs=(P("data", None, None), P("data", None, None), P("stage", None, None, "model"), P("stage", None, "model", None)),
        out_specs=(P(("data", "stage"), None, None, "model"), P(("data", "stage"), None, "model", None), P("data")),
        check_vma=False,
    )
```

time: 6660 us -> 2800 us (0.42)
  waiting for transfers between devices: 3550 us -> 0 us
  Pallas kernels: 0 us -> 2650 us
  matrix products: 2590 us -> 103 us
  other arithmetic: 329 us -> 7.49 us
    psum x30 -> x0, waiting for transfers between devices: 3550 us -> none  [the longest x15 2240 us: fwd_tick(): lax.psum(part_sum, 'model')]
    pallas_call x0 -> x1, Pallas kernels: none -> 2650 us  [run_pipeline(): pl.pallas_call(pipeline_kernel, out_shape=out_shape, in_specs=[hbm] * 4,...]
    dot_general x90 -> x2, matrix products: 2590 us -> 103 us  [dot_tn(): lax.dot_general(a, b, (((0,), (0,)), ((), ())), preferred_element_type=F32)]
    dynamic_update_slice x30 -> x0, other arithmetic: 160 us -> none  [stage_step(): lax.scan(fwd_tick, fwd_init, jnp.arange(num_ticks))]
    convert_element_type x15 -> x0, other arithmetic: 71.5 us -> none  [bwd_tick(): (grad_h.astype(jnp.float32) + lax.psum(part_sum, 'model')).astype(jnp.bfl...]
  transfers between devices with their start and end apart: 60 -> 0, of which waited for: 30 -> 0; matrix products, arithmetic and copies ran while one was open for 18% -> 0% of each run, Pallas kernels for 0% -> 0%
where the time goes in v1:
time: 2800 us; the launch traced here: 2790 us
  Pallas kernels  2650 us (95%)
  matrix products  103 us (4%)
    pallas_call x1, Pallas kernels, run_pipeline(): pl.pallas_call(pipeline_kernel, out_shape=out_shape, in_specs=[hbm] * 4,...  2650 us
    dot_general x2, matrix products, dot_tn(): lax.dot_general(a, b, (((0,), (0,)), ((), ())), preferred_element_type=F32)  103 us

profile of v1, /device:TPU:0, one launch (start us, length us, event | category | flops | bytes accessed | tf_op | source)
XLA Modules:
  0.0 2792.5 jit_solution(3874889229353151822)
XLA Ops:
  0.6 2651.6 %pipeline.1 = (bf16[6144,2560]{1,0:T(8,128)(2,1)}, bf16[6144,2560]{1,0:T(8,128)(2,1)}, bf16[6144,5120]{1,0:T(8,128)(2,1)}, bf16[6144,5120]{1,0:T(8,128)(2,1)}, b...) custom-call(bf16[6144,2560]{1,0:T(8,128)(2,1)} %bitcast.12, ...), custom_call_target="tpu_custom_call" | custom-call | tf_op jit(solution)/shard_map/pipeline/pallas_call | solution.py:473
  2652.2 51.8 %add_bitcast_fusion = f32[1,1,5120,2560]{3,2,1,0:T(8,128)} fusion(f32[5120,2560]{1,0:T(8,128)} %get-tuple-element.13, bf16[6144,5120]{1,0:T(8,128)(2,1)} %get-tuple-element.14, bf16[6144,2560]{1,0:T(8,128)(2,1)} %get-tuple-element.15), kind=kOutput, calls=%fused_computation | convolution fusion | flops 26856652800 | bytes 120586240 | tf_op jit(solution)/shard_map/dot_general | solution.py:36
  2704.0 5.2 slice.18
  2709.2 6.9 bitcast_select_fusion
  2716.1 0.0 copy-start
  2716.1 51.6 %add_bitcast_fusion.1 = f32[1,1,2560,5120]{3,2,1,0:T(8,128)} fusion(f32[2560,5120]{1,0:T(8,128)} %get-tuple-element.10, bf16[1024,2560]{1,0:T(8,128)(2,1)} %bitcast_select_fusion, bf16[6144,5120]{1,0:T(8,128)(2,1)} %get-tuple-element.12), kind=kOutput, calls=%fused_computation.1 | convolution fusion | flops 26856652800 | bytes 120586240 | tf_op jit(solution)/shard_map/dot_general | solution.py:36
  2767.7 0.0 copy-done
  2767.7 0.6 reduce_sum.9
  2768.3 22.4 psum.7
Async XLA Ops:
  2716.1 51.6 %copy-start = (f32[8,128]{1,0:T(8,128)S(1)}, f32[8,128]{1,0:T(8,128)}, u32[]{:S(2)}) copy-start(f32[8,128]{1,0:T(8,128)} %get-tuple-element.16) | copy-start | bytes 12292

commit v2 on v1

--- a/solution.py
+++ b/solution.py
@@ -19,6 +19,7 @@
 N_GRP = N_MB // GROUP - 1
 GTOK = GROUP * TOK
 N_ELEM = N_MB * TOK * DIM
+RELAY0 = 3
 MESH = pl.DeviceIdType.MESH
 BF = jnp.bfloat16
 F32 = jnp.float32
@@ -47,17 +48,17 @@
 
 def pipeline_kernel(
     x_in, tgt, w1, w2,
-    x_all, e_all, u_all, a_all, g_all, rsf, rsb, acc1, acc2, loss,
-    xbuf, w1buf, w2buf, ubuf, abuf, gbuf, uin, accf, accb, rsv, res, tbuf, yf, yb, wide, narrow, wtile,
+    x_all, e_all, u_all, a_all, g_all, rsf, rsb, fwd, acc1, acc2, loss,
+    xbuf, w1buf, w2buf, ubuf, abuf, gbuf, uin, accf, accb, rsv, res, tbuf, yf, yb, wide, narrow, wtile, lsum, lrx,
     w_sem, x_sem, uo_sem, ao_sem, go_sem, ui_sem, p_sem, wd_sem, wn_sem, wl_sem, ws_sem,
-    xr_sem, er_sem, rf_sem, rb_sem, sf_sem, sb_sem, yf_sem, yb_sem,
+    xr_sem, er_sem, rf_sem, rb_sem, sf_sem, sb_sem, yf_sem, yb_sem, fr_sem, fs_sem, ls_sem, lr_sem,
 ):
     my = lax.axis_index("model")
     st = lax.axis_index("stage")
     other = 1 - my
     last = st == 3
     first = st == 0
-    warm = jnp.where(st == 0, 16, jnp.where(st == 1, 12, jnp.where(st == 2, 6, 2)))
+    warm = jnp.where(st == 0, 16, jnp.where(st == 1, 10, jnp.where(st == 2, 5, 2)))
     partner = {"model": other}
     nxt = jnp.minimum(st + 1, 3)
     prv = jnp.maximum(st - 1, 0)
@@ -106,6 +107,29 @@
             half_copy(yf, slot, x_all, m, my, yf_sem, 1, xr_sem, {"model": other, "stage": nxt}),
         )
 
+    def fwd_rows(m):
+        return pl.ds(pl.multiple_of(m * HALF, HALF), HALF)
+
+    def fwd_send(m, slot):
+        return pltpu.make_async_remote_copy(
+            src_ref=yf.at[slot],
+            dst_ref=fwd.at[fwd_rows(m), :],
+            send_sem=yf_sem.at[slot, 1],
+            recv_sem=fr_sem.at[m],
+            device_id=partner,
+            device_id_type=MESH,
+        )
+
+    def relay_copy(m):
+        return pltpu.make_async_remote_copy(
+            src_ref=fwd.at[fwd_rows(m), :],
+            dst_ref=x_all.at[rows_of(m, other), :],
+            send_sem=fs_sem.at[lax.rem(m, 2)],
+            recv_sem=xr_sem.at[m, other],
+            device_id={"model": my, "stage": nxt},
+            device_id_type=MESH,
+        )
+
     def yl_own(m, slot):
         return pltpu.make_async_copy(yf.at[slot], e_all.at[rows_of(m, my), :], er_sem.at[m, my])
 
@@ -140,6 +164,12 @@
         @pl.when(first)
         def _():
             load_x(x_in, m)
+
+            @pl.when(m >= N_GRP * GROUP)
+            def _():
+                cp = pltpu.make_async_copy(xbuf, x_all.at[mb_rows(m), :], x_sem)
+                cp.start()
+                cp.wait()
 
         @pl.when(jnp.logical_not(first))
         def _():
@@ -225,8 +255,17 @@
         @pl.when(jnp.logical_not(last))
         def _():
             yf[slot] = y
-            for cp in yf_pair(m, slot):
-                cp.start()
+            own, cross = yf_pair(m, slot)
+            own.start()
+            by_pair = jnp.logical_and(st == 1, m >= RELAY0)
+
+            @pl.when(by_pair)
+            def _():
+                fwd_send(m, slot).start()
+
+            @pl.when(jnp.logical_not(by_pair))
+            def _():
+                cross.start()
 
         @pl.when(last)
         def _():
@@ -236,9 +275,40 @@
             part = sq[:, 0:128]
             for c in range(1, DIM // 128):
                 part = part + sq[:, c * 128 : (c + 1) * 128]
-            loss[...] += jnp.sum(part.reshape(HALF // 8, 8, 128), axis=0)
+            lsum[...] += jnp.sum(part.reshape(HALF // 8, 8, 128), axis=0)
             yl_own(m, slot).start()
             yl_send(m, slot).start()
+
+            @pl.when(m == N_MB - 1)
+            def _():
+                pltpu.make_async_copy(lsum, lrx.at[my], lr_sem.at[my]).start()
+                for cond, cp in loss_sends():
+                    pl.when(cond)(cp.start)
+
+    def relay(m):
+        @pl.when(jnp.logical_and(st == 1, jnp.logical_and(m >= RELAY0, m < N_MB)))
+        def _():
+            ref = fwd.at[fwd_rows(m), :]
+            pltpu.make_async_copy(ref, ref, fr_sem.at[m]).wait()
+
+            @pl.when(m >= RELAY0 + 2)
+            def _():
+                relay_copy(m - 2).wait_send()
+
+            relay_copy(m).start()
+
+    def loss_sends():
+        for y in range(2):
+            for s in range(4):
+                cp = pltpu.make_async_remote_copy(
+                    src_ref=lsum,
+                    dst_ref=lrx.at[my],
+                    send_sem=ls_sem.at[y * 4 + s],
+                    recv_sem=lr_sem.at[my],
+                    device_id={"model": y, "stage": s},
+                    device_id_type=MESH,
+                )
+                yield (True if s < 3 else my != y), cp
 
     def backward(m):
         slot_m = lax.rem(m, 2)
@@ -394,7 +464,7 @@
 
         wait_store(0)
 
-    loss[...] = jnp.zeros((8, 128), F32)
+    lsum[...] = jnp.zeros((8, 128), F32)
     for cp in w_copies(0, 0):
         cp.start()
 
@@ -416,6 +486,10 @@
         def _():
             forward_post(p)
 
+        @pl.when(b_on)
+        def _():
+            relay(k - 2)
+
         @pl.when(f_on)
         def _():
             forward(k)
@@ -424,6 +498,10 @@
         def _():
             forward_post(p)
 
+        @pl.when(jnp.logical_not(b_on))
+        def _():
+            relay(k - 2)
+
         @pl.when(jnp.logical_and(pb_on, f_on))
         def _():
             backward_post(b)
@@ -435,6 +513,10 @@
         @pl.when(jnp.logical_and(pb_on, jnp.logical_not(f_on)))
         def _():
             backward_post(b)
+
+    for half in range(2):
+        pltpu.make_async_copy(lsum, lrx.at[half], lr_sem.at[half]).wait()
+    loss[...] = lrx[0] + lrx[1]
 
     for cp in w_copies(0, 0):
         cp.wait()
@@ -457,6 +539,15 @@
         def _():
             for cp in yf_pair(m, slot):
                 cp.wait_send()
+
+        @pl.when(st == 1)
+        def _():
+            relay_copy(m).wait_send()
+
+    @pl.when(last)
+    def _():
+        for cond, cp in loss_sends():
+            pl.when(cond)(cp.wait_send)
 
 
 def run_pipeline(x_in, tgt, w1, w2):
@@ -466,7 +557,7 @@
     shapes = [
         ((tokens, DIM), BF), ((tokens, DIM), BF),
         ((tokens, HID), BF), ((tokens, HID), BF), ((tokens, HID), BF),
-        ((tokens // 2, DIM), F32), ((tokens // 2, DIM), F32),
+        ((tokens // 2, DIM), F32), ((tokens // 2, DIM), F32), ((tokens // 2, DIM), BF),
         ((DIM, HID), F32), ((HID, DIM), F32),
     ]
     out_shape = [jax.ShapeDtypeStruct(s, d) for s, d in shapes] + [jax.ShapeDtypeStruct((8, 128), F32)]
@@ -474,7 +565,7 @@
         pipeline_kernel,
         out_shape=out_shape,
         in_specs=[hbm] * 4,
-        out_specs=[hbm] * 9 + [pl.BlockSpec(memory_space=pltpu.VMEM)],
+        out_specs=[hbm] * 10 + [pl.BlockSpec(memory_space=pltpu.VMEM)],
         scratch_shapes=[
             pltpu.VMEM((TOK, DIM), BF),
             pltpu.VMEM((2, DIM, HB), BF),
@@ -493,12 +584,36 @@
             pltpu.VMEM((GTOK, DIM), BF),
             pltpu.VMEM((2, GTOK, HB), BF),
             pltpu.VMEM((2, HB, DIM), F32),
+            pltpu.VMEM((8, 128), F32),
+            pltpu.VMEM((2, 8, 128), F32),
             dma((2, 2)), dma, dma((2,)), dma((2,)), dma((2,)), dma((2,)), dma((3,)), dma, dma((2,)), dma((2,)), dma((2,)),
             dma((N_MB, 2)), dma((N_MB, 2)), dma((N_MB,)), dma((N_MB,)), dma((2,)), dma((2,)), dma((2, 2)), dma((2, 2)),
+            dma((N_MB,)), dma((2,)), dma((8,)), dma((2,)),
         ],
         compiler_params=pltpu.CompilerParams(vmem_limit_bytes=66_000_000, has_side_effects=True),
         name="pipeline",
     )(x_in, tgt, w1, w2)
+
+
+def add_tail(acc, left, right, n_row_blk, n_col_blk, name):
+    rows = TOK
+
+    def body(acc_ref, l_ref, r_ref, o_ref):
+        o_ref[...] = acc_ref[...] + dot_tn(l_ref[...], r_ref[...])
+
+    return pl.pallas_call(
+        body,
+        grid=(n_col_blk, n_row_blk),
+        in_specs=[
+            pl.BlockSpec((rows, DIM), lambda c, r: (r, c)),
+            pl.BlockSpec((GTOK, rows), lambda c, r: (N_GRP, r)),
+            pl.BlockSpec((GTOK, DIM), lambda c, r: (N_GRP, c)),
+        ],
+        out_specs=pl.BlockSpec((rows, DIM), lambda c, r: (r, c)),
+        out_shape=jax.ShapeDtypeStruct(acc.shape, F32),
+        compiler_params=pltpu.CompilerParams(vmem_limit_bytes=56_000_000),
+        name=name,
+    )(acc, left, right)
 
 
 def solution(mesh):
@@ -506,12 +621,10 @@
         tokens = N_MB * TOK
         x_in = inputs.reshape(tokens, DIM)
         tgt = targets.reshape(tokens, DIM)
-        x_all, e_all, _, a_all, g_all, _, _, acc1, acc2, loss = run_pipeline(x_in, tgt, w_in[0, 0], w_out[0, 0])
-        tail = slice(N_GRP * GTOK, tokens)
-        x_tail = jnp.where(lax.axis_index("stage") == 0, x_in[tail], x_all[tail])
-        grad_in = acc1 + dot_tn(x_tail, g_all[tail])
-        grad_out = acc2 + dot_tn(a_all[tail], e_all[tail])
-        total = lax.psum(jnp.sum(loss), ("model", "stage")) * (0.5 / N_ELEM)
+        x_all, e_all, _, a_all, g_all, _, _, _, acc1, acc2, loss = run_pipeline(x_in, tgt, w_in[0, 0], w_out[0, 0])
+        grad_in = add_tail(acc1, x_all, g_all, DIM // TOK, HID // DIM, "tail_in")
+        grad_out = add_tail(acc2, a_all, e_all, HID // TOK, 1, "tail_out")
+        total = jnp.sum(loss) * (0.5 / N_ELEM)
         return grad_in[None, None], grad_out[None, None], jnp.reshape(total, (1,))
 
     return jax.shard_map(

time: 2800 us -> 2700 us (0.964)
  matrix products: 103 us -> 0 us
  Pallas kernels: 2650 us -> 2690 us
    pallas_call x0 -> x2, Pallas kernels: none -> 111 us  [add_tail(): pl.pallas_call(body, grid=(n_col_blk, n_row_blk), in_specs=[pl.BlockSpec(...]
    dot_general x2 -> x0, matrix products: 103 us -> none  [dot_tn(): lax.dot_general(a, b, (((0,), (0,)), ((), ())), preferred_element_type=F32)]
    pallas_call x1, Pallas kernels: 2650 us -> 2580 us  [run_pipeline(): pl.pallas_call(pipeline_kernel, out_shape=out_shape, in_specs=[hbm] * 4,...]
where the time goes in v2:
time: 2700 us
  Pallas kernels  2690 us (100%)
    pallas_call x1, Pallas kernels, run_pipeline(): pl.pallas_call(pipeline_kernel, out_shape=out_shape, in_specs=[hbm] * 4,...  2580 us
    pallas_call x2, Pallas kernels, add_tail(): pl.pallas_call(body, grid=(n_col_blk, n_row_blk), in_specs=[pl.BlockSpec(...  111 us

profile of v2, /device:TPU:0, one launch (start us, length us, event | category | flops | bytes accessed | tf_op | source)
XLA Modules:
  0.0 2697.3 jit_solution(3140387129238927913)
XLA Ops:
  0.6 2582.6 %pipeline.1 = (bf16[6144,2560]{1,0:T(8,128)(2,1)}, bf16[6144,2560]{1,0:T(8,128)(2,1)}, bf16[6144,5120]{1,0:T(8,128)(2,1)}, bf16[6144,5120]{1,0:T(8,128)(2,1)}, b...) custom-call(bf16[6144,2560]{1,0:T(8,128)(2,1)} %bitcast.9, ...), custom_call_target="tpu_custom_call" | custom-call | tf_op jit(solution)/shard_map/pipeline/pallas_call | solution.py:564
  2583.3 1.3 reduce_sum.9
  2585.2 56.6 %tail_in.1 = f32[2560,5120]{1,0:T(8,128)} custom-call(f32[2560,5120]{1,0:T(8,128)} %get-tuple-element.10.acc_ref, bf16[6144,2560]{1,0:T(8,128)(2,1)} %get-tuple-element.11.l_ref, bf16[6144,5120]{1,0:T(8,128)(2,1)} %get-tuple-element.12.r_ref), custom_call_target="tpu_custom_call" | custom-call | tf_op jit(solution)/shard_map/tail_in/pallas_call | solution.py:604
  2641.8 54.4 %tail_out.1 = f32[5120,2560]{1,0:T(8,128)} custom-call(f32[5120,2560]{1,0:T(8,128)} %get-tuple-element.13.acc_ref, bf16[6144,5120]{1,0:T(8,128)(2,1)} %get-tuple-element.14.l_ref, bf16[6144,2560]{1,0:T(8,128)(2,1)} %get-tuple-element.15.r_ref), custom_call_target="tpu_custom_call" | custom-call | tf_op jit(solution)/shard_map/tail_out/pallas_call | solution.py:604

commit v3 on v2

--- a/solution.py
+++ b/solution.py
@@ -15,6 +15,7 @@
 HID = 5120
 HB = 512
 N_BLK = HID // HB
+W_SLOTS = 3
 GROUP = 4
 N_GRP = N_MB // GROUP - 1
 GTOK = GROUP * TOK
@@ -158,7 +159,17 @@
         cp.start()
         cp.wait()
 
-    def forward(m):
+    def next_weights(count, j):
+        at = count * N_BLK + j
+        slot = lax.rem(at, W_SLOTS)
+        for cp in w_copies(j, slot):
+            cp.wait()
+        ahead = W_SLOTS - 1
+        for cp in w_copies(lax.rem(j + ahead, N_BLK), lax.rem(at + ahead, W_SLOTS)):
+            cp.start()
+        return slot
+
+    def forward(m, count):
         slot_m = lax.rem(m, 2)
 
         @pl.when(first)
@@ -183,17 +194,14 @@
         @pl.loop(0, N_BLK)
         def _(j):
             slot = lax.rem(j, 2)
-            for cp in w_copies(j, slot):
-                cp.wait()
-            for cp in w_copies(lax.rem(j + 1, N_BLK), 1 - slot):
-                cp.start()
+            ws = next_weights(count, j)
 
             @pl.when(m * N_BLK + j >= 2)
             def _():
                 out_copy(ubuf, slot, u_all, m, j, uo_sem).wait()
                 out_copy(abuf, slot, a_all, m, j, ao_sem).wait()
 
-            ubuf[slot] = dot_nn(xbuf[...], w1buf[slot]).astype(BF)
+            ubuf[slot] = dot_nn(xbuf[...], w1buf[ws]).astype(BF)
             abuf[slot] = gelu(ubuf[slot].astype(F32)).astype(BF)
             out_copy(ubuf, slot, u_all, m, j, uo_sem).start()
             out_copy(abuf, slot, a_all, m, j, ao_sem).start()
@@ -202,7 +210,7 @@
             def _():
                 accf[slot_m] = jnp.zeros((TOK, DIM), F32)
 
-            accf[slot_m] += dot_nn(abuf[slot], w2buf[slot])
+            accf[slot_m] += dot_nn(abuf[slot], w2buf[ws])
 
         rs_copy(accf, slot_m, rsf, m, sf_sem, rf_sem).start()
 
@@ -310,7 +318,7 @@
                 )
                 yield (True if s < 3 else my != y), cp
 
-    def backward(m):
+    def backward(m, count):
         slot_m = lax.rem(m, 2)
         u_load(m, 0, 0).start()
         wait_in(e_all, m, er_sem)
@@ -323,10 +331,7 @@
         @pl.loop(0, N_BLK)
         def _(j):
             slot = lax.rem(j, 2)
-            for cp in w_copies(j, slot):
-                cp.wait()
-            for cp in w_copies(lax.rem(j + 1, N_BLK), 1 - slot):
-                cp.start()
+            ws = next_weights(count, j)
             u_load(m, j, slot).wait()
 
             @pl.when(j + 1 < N_BLK)
@@ -337,7 +342,7 @@
             def _():
                 out_copy(gbuf, slot, g_all, m, j, go_sem).wait()
 
-            q = dot_nt(xbuf[...], w2buf[slot]).astype(BF)
+            q = dot_nt(xbuf[...], w2buf[ws]).astype(BF)
             gbuf[slot] = (gelu_slope(uin[slot].astype(F32)) * q.astype(F32)).astype(BF)
             out_copy(gbuf, slot, g_all, m, j, go_sem).start()
 
@@ -347,7 +352,7 @@
                 def _():
                     accb[slot_m] = jnp.zeros((TOK, DIM), F32)
 
-                accb[slot_m] += dot_nt(gbuf[slot], w1buf[slot])
+                accb[slot_m] += dot_nt(gbuf[slot], w1buf[ws])
 
         @pl.when(jnp.logical_not(first))
         def _():
@@ -367,7 +372,7 @@
         for cp in yb_pair(m, slot):
             cp.start()
 
-    def weight_step(v):
+    def weight_ops(v):
         grp = v // GROUP
         quart = lax.rem(v, GROUP)
         rows = pl.ds(pl.multiple_of(grp * GTOK, GTOK), GTOK)
@@ -382,31 +387,35 @@
             def _():
                 fn1(cols(t), cols(quart - 2, DIM))
 
-        def start_narrow(t, slot):
+        def start_tile(t):
+            n_slot = lax.rem(t, 2)
+            slot = lax.rem(t, 3)
+
             def fn2(blk):
-                pltpu.make_async_copy(a_all.at[rows, blk], narrow.at[slot], wn_sem.at[slot]).start()
+                pltpu.make_async_copy(a_all.at[rows, blk], narrow.at[n_slot], wn_sem.at[n_slot]).start()
+
+                @pl.when(grp > 0)
+                def _():
+                    pltpu.make_async_copy(acc2.at[blk, :], wtile.at[slot], wl_sem.at[slot]).start()
 
             def fn1(dblk, half):
                 @pl.when(first)
                 def _():
-                    pltpu.make_async_copy(x_in.at[rows, dblk], narrow.at[slot], wn_sem.at[slot]).start()
+                    pltpu.make_async_copy(x_in.at[rows, dblk], narrow.at[n_slot], wn_sem.at[n_slot]).start()
 
                 @pl.when(jnp.logical_not(first))
                 def _():
-                    pltpu.make_async_copy(x_all.at[rows, dblk], narrow.at[slot], wn_sem.at[slot]).start()
+                    pltpu.make_async_copy(x_all.at[rows, dblk], narrow.at[n_slot], wn_sem.at[n_slot]).start()
+
+                @pl.when(grp > 0)
+                def _():
+                    pltpu.make_async_copy(acc1.at[dblk, half], wtile.at[slot], wl_sem.at[slot]).start()
 
             on_tile(t, fn2, fn1)
 
-        def start_tile(t, slot):
-            def fn2(blk):
-                pltpu.make_async_copy(acc2.at[blk, :], wtile.at[slot], wl_sem.at[slot]).start()
-
-            def fn1(dblk, half):
-                pltpu.make_async_copy(acc1.at[dblk, half], wtile.at[slot], wl_sem.at[slot]).start()
-
-            on_tile(t, fn2, fn1)
-
-        def start_store(t, slot):
+        def start_store(t):
+            slot = lax.rem(t, 3)
+
             def fn2(blk):
                 pltpu.make_async_copy(wtile.at[slot], acc2.at[blk, :], ws_sem.at[slot]).start()
 
@@ -418,55 +427,55 @@
         def wait_store(slot):
             pltpu.make_async_copy(wtile.at[slot], acc2.at[pl.ds(0, HB), :], ws_sem.at[slot]).wait()
 
-        @pl.when(out2)
-        def _():
-            pltpu.make_async_copy(e_all.at[rows, :], wide, wd_sem).start()
-
-        @pl.when(jnp.logical_not(out2))
-        def _():
-            pltpu.make_async_copy(g_all.at[rows, cols(quart - 2, DIM)], wide, wd_sem).start()
-
-        start_narrow(0, 0)
-
-        @pl.when(grp > 0)
-        def _():
-            start_tile(0, 0)
-
-        pltpu.make_async_copy(e_all.at[rows, :], wide, wd_sem).wait()
-
-        @pl.loop(0, 5)
-        def _(t):
-            slot = lax.rem(t, 2)
-            pltpu.make_async_copy(a_all.at[rows, pl.ds(0, HB)], narrow.at[slot], wn_sem.at[slot]).wait()
-
-            @pl.when(grp > 0)
-            def _():
-                pltpu.make_async_copy(acc2.at[pl.ds(0, HB), :], wtile.at[slot], wl_sem.at[slot]).wait()
-
-            @pl.when(t >= 1)
-            def _():
-                wait_store(1 - slot)
-
-            @pl.when(t < 4)
-            def _():
-                start_narrow(t + 1, 1 - slot)
+        def start():
+            @pl.when(out2)
+            def _():
+                pltpu.make_async_copy(e_all.at[rows, :], wide, wd_sem).start()
+
+            @pl.when(jnp.logical_not(out2))
+            def _():
+                pltpu.make_async_copy(g_all.at[rows, cols(quart - 2, DIM)], wide, wd_sem).start()
+
+            start_tile(0)
+
+        def run():
+            pltpu.make_async_copy(e_all.at[rows, :], wide, wd_sem).wait()
+
+            @pl.loop(0, 5)
+            def _(t):
+                slot = lax.rem(t, 3)
+                n_slot = lax.rem(t, 2)
+
+                @pl.when(t >= 2)
+                def _():
+                    wait_store(lax.rem(t + 1, 3))
+
+                @pl.when(t < 4)
+                def _():
+                    start_tile(t + 1)
+
+                pltpu.make_async_copy(a_all.at[rows, pl.ds(0, HB)], narrow.at[n_slot], wn_sem.at[n_slot]).wait()
 
                 @pl.when(grp > 0)
                 def _():
-                    start_tile(t + 1, 1 - slot)
-
-            @pl.when(grp == 0)
-            def _():
-                wtile[slot] = jnp.zeros((HB, DIM), F32)
-
-            wtile[slot] += dot_tn(narrow[slot], wide[...])
-            start_store(t, slot)
-
-        wait_store(0)
+                    pltpu.make_async_copy(acc2.at[pl.ds(0, HB), :], wtile.at[slot], wl_sem.at[slot]).wait()
+
+                @pl.when(grp == 0)
+                def _():
+                    wtile[slot] = jnp.zeros((HB, DIM), F32)
+
+                wtile[slot] += dot_tn(narrow[n_slot], wide[...])
+                start_store(t)
+
+            wait_store(0)
+            wait_store(1)
+
+        return start, run
 
     lsum[...] = jnp.zeros((8, 128), F32)
-    for cp in w_copies(0, 0):
-        cp.start()
+    for j in range(W_SLOTS - 1):
+        for cp in w_copies(j, j):
+            cp.start()
 
     @pl.loop(0, N_MB + warm)
     def _(k):
@@ -480,7 +489,7 @@
 
         @pl.when(b_on)
         def _():
-            backward(b)
+            backward(b, b + jnp.minimum(k, N_MB))
 
         @pl.when(jnp.logical_and(b_on, p_on))
         def _():
@@ -490,9 +499,13 @@
         def _():
             relay(k - 2)
 
+        @pl.when(v >= 0)
+        def _():
+            weight_ops(v)[0]()
+
         @pl.when(f_on)
         def _():
-            forward(k)
+            forward(k, k + jnp.maximum(b + 1, 0))
 
         @pl.when(jnp.logical_and(jnp.logical_not(b_on), p_on))
         def _():
@@ -508,7 +521,7 @@
 
         @pl.when(v >= 0)
         def _():
-            weight_step(v)
+            weight_ops(v)[1]()
 
         @pl.when(jnp.logical_and(pb_on, jnp.logical_not(f_on)))
         def _():
@@ -518,8 +531,9 @@
         pltpu.make_async_copy(lsum, lrx.at[half], lr_sem.at[half]).wait()
     loss[...] = lrx[0] + lrx[1]
 
-    for cp in w_copies(0, 0):
-        cp.wait()
+    for j in range(W_SLOTS - 1):
+        for cp in w_copies(j, (2 * N_MB * N_BLK + j) % W_SLOTS):
+            cp.wait()
     for m in (N_MB - 2, N_MB - 1):
         slot = m % 2
         out_copy(gbuf, slot, g_all, m, 0, go_sem).wait()
@@ -568,8 +582,8 @@
         out_specs=[hbm] * 10 + [pl.BlockSpec(memory_space=pltpu.VMEM)],
         scratch_shapes=[
             pltpu.VMEM((TOK, DIM), BF),
-            pltpu.VMEM((2, DIM, HB), BF),
-            pltpu.VMEM((2, HB, DIM), BF),
+            pltpu.VMEM((W_SLOTS, DIM, HB), BF),
+            pltpu.VMEM((W_SLOTS, HB, DIM), BF),
             pltpu.VMEM((2, TOK, HB), BF),
             pltpu.VMEM((2, TOK, HB), BF),
             pltpu.VMEM((2, TOK, HB), BF),
@@ -583,10 +597,10 @@
             pltpu.VMEM((2, HALF, DIM), BF),
             pltpu.VMEM((GTOK, DIM), BF),
             pltpu.VMEM((2, GTOK, HB), BF),
-            pltpu.VMEM((2, HB, DIM), F32),
+            pltpu.VMEM((3, HB, DIM), F32),
             pltpu.VMEM((8, 128), F32),
             pltpu.VMEM((2, 8, 128), F32),
-            dma((2, 2)), dma, dma((2,)), dma((2,)), dma((2,)), dma((2,)), dma((3,)), dma, dma((2,)), dma((2,)), dma((2,)),
+            dma((W_SLOTS, 2)), dma, dma((2,)), dma((2,)), dma((2,)), dma((2,)), dma((3,)), dma, dma((2,)), dma((3,)), dma((3,)),
             dma((N_MB, 2)), dma((N_MB, 2)), dma((N_MB,)), dma((N_MB,)), dma((2,)), dma((2,)), dma((2, 2)), dma((2, 2)),
             dma((N_MB,)), dma((2,)), dma((8,)), dma((2,)),
         ],
@@ -596,7 +610,7 @@
 
 
 def add_tail(acc, left, right, n_row_blk, n_col_blk, name):
-    rows = TOK
+    rows = HB
 
     def body(acc_ref, l_ref, r_ref, o_ref):
         o_ref[...] = acc_ref[...] + dot_tn(l_ref[...], r_ref[...])
@@ -622,8 +636,8 @@
         x_in = inputs.reshape(tokens, DIM)
         tgt = targets.reshape(tokens, DIM)
         x_all, e_all, _, a_all, g_all, _, _, _, acc1, acc2, loss = run_pipeline(x_in, tgt, w_in[0, 0], w_out[0, 0])
-        grad_in = add_tail(acc1, x_all, g_all, DIM // TOK, HID // DIM, "tail_in")
-        grad_out = add_tail(acc2, a_all, e_all, HID // TOK, 1, "tail_out")
+        grad_in = add_tail(acc1, x_all, g_all, DIM // HB, HID // DIM, "tail_in")
+        grad_out = add_tail(acc2, a_all, e_all, HID // HB, 1, "tail_out")
         total = jnp.sum(loss) * (0.5 / N_ELEM)
         return grad_in[None, None], grad_out[None, None], jnp.reshape(total, (1,))
 

time: 2700 us -> 2390 us (0.89)
  Pallas kernels: 2690 us -> 2390 us
    pallas_call x1, Pallas kernels: 2580 us -> 2290 us  [run_pipeline(): pl.pallas_call(pipeline_kernel, out_shape=out_shape, in_specs=[hbm] * 4,...]
where the time goes in v3:
time: 2390 us
  Pallas kernels  2390 us (100%)
    pallas_call x1, Pallas kernels, run_pipeline(): pl.pallas_call(pipeline_kernel, out_shape=out_shape, in_specs=[hbm] * 4,...  2290 us
    pallas_call x2, Pallas kernels, add_tail(): pl.pallas_call(body, grid=(n_col_blk, n_row_blk), in_specs=[pl.BlockSpec(...  100 us

profile of v3, /device:TPU:0, one launch (start us, length us, event | category | flops | bytes accessed | tf_op | source)
XLA Modules:
  0.0 2390.2 jit_solution(9913693280197689063)
XLA Ops:
  0.6 2286.1 %pipeline.1 = (bf16[6144,2560]{1,0:T(8,128)(2,1)}, bf16[6144,2560]{1,0:T(8,128)(2,1)}, bf16[6144,5120]{1,0:T(8,128)(2,1)}, bf16[6144,5120]{1,0:T(8,128)(2,1)}, b...) custom-call(bf16[6144,2560]{1,0:T(8,128)(2,1)} %bitcast.9, ...), custom_call_target="tpu_custom_call" | custom-call | tf_op jit(solution)/shard_map/pipeline/pallas_call | solution.py:578
  2286.7 1.3 reduce_sum.9
  2288.7 49.9 %tail_in.1 = f32[2560,5120]{1,0:T(8,128)} custom-call(f32[2560,5120]{1,0:T(8,128)} %get-tuple-element.10.acc_ref, bf16[6144,2560]{1,0:T(8,128)(2,1)} %get-tuple-element.11.l_ref, bf16[6144,5120]{1,0:T(8,128)(2,1)} %get-tuple-element.12.r_ref), custom_call_target="tpu_custom_call" | custom-call | tf_op jit(solution)/shard_map/tail_in/pallas_call | solution.py:618
  2338.6 50.5 %tail_out.1 = f32[5120,2560]{1,0:T(8,128)} custom-call(f32[5120,2560]{1,0:T(8,128)} %get-tuple-element.13.acc_ref, bf16[6144,5120]{1,0:T(8,128)(2,1)} %get-tuple-element.14.l_ref, bf16[6144,2560]{1,0:T(8,128)(2,1)} %get-tuple-element.15.r_ref), custom_call_target="tpu_custom_call" | custom-call | tf_op jit(solution)/shard_map/tail_out/pallas_call | solution.py:618

commit v4 on v3

--- a/solution.py
+++ b/solution.py
@@ -21,6 +21,8 @@
 GTOK = GROUP * TOK
 N_ELEM = N_MB * TOK * DIM
 RELAY0 = 3
+RELAY3 = 10
+LEAD3 = 3
 MESH = pl.DeviceIdType.MESH
 BF = jnp.bfloat16
 F32 = jnp.float32
@@ -121,13 +123,29 @@
             device_id_type=MESH,
         )
 
-    def relay_copy(m):
+    def relay_copy(m, dst, recv, to):
         return pltpu.make_async_remote_copy(
             src_ref=fwd.at[fwd_rows(m), :],
-            dst_ref=x_all.at[rows_of(m, other), :],
+            dst_ref=dst.at[rows_of(m, other), :],
             send_sem=fs_sem.at[lax.rem(m, 2)],
-            recv_sem=xr_sem.at[m, other],
-            device_id={"model": my, "stage": nxt},
+            recv_sem=recv.at[m, other],
+            device_id={"model": my, "stage": to},
+            device_id_type=MESH,
+        )
+
+    def relay_x(m):
+        return relay_copy(m, x_all, xr_sem, 2)
+
+    def relay_e(m):
+        return relay_copy(m, e_all, er_sem, 2)
+
+    def far_send(m, slot):
+        return pltpu.make_async_remote_copy(
+            src_ref=yb.at[slot],
+            dst_ref=fwd.at[fwd_rows(m), :],
+            send_sem=yb_sem.at[slot, 1],
+            recv_sem=fr_sem.at[m],
+            device_id={"model": other, "stage": 0},
             device_id_type=MESH,
         )
 
@@ -293,17 +311,25 @@
                 for cond, cp in loss_sends():
                     pl.when(cond)(cp.start)
 
+    def pass_on(m, base, copy):
+        ref = fwd.at[fwd_rows(m), :]
+        pltpu.make_async_copy(ref, ref, fr_sem.at[m]).wait()
+
+        @pl.when(m >= base + 2)
+        def _():
+            copy(m - 2).wait_send()
+
+        copy(m).start()
+
     def relay(m):
         @pl.when(jnp.logical_and(st == 1, jnp.logical_and(m >= RELAY0, m < N_MB)))
         def _():
-            ref = fwd.at[fwd_rows(m), :]
-            pltpu.make_async_copy(ref, ref, fr_sem.at[m]).wait()
-
-            @pl.when(m >= RELAY0 + 2)
-            def _():
-                relay_copy(m - 2).wait_send()
-
-            relay_copy(m).start()
+            pass_on(m, RELAY0, relay_x)
+
+    def relay_back(m):
+        @pl.when(jnp.logical_and(first, jnp.logical_and(m >= RELAY3, m < N_MB)))
+        def _():
+            pass_on(m, RELAY3, relay_e)
 
     def loss_sends():
         for y in range(2):
@@ -369,8 +395,17 @@
                 cp.wait_send()
 
         yb[slot] = (res[...].astype(F32) + (accb[slot, half_rows(my), :] + rsv[...])).astype(BF)
-        for cp in yb_pair(m, slot):
-            cp.start()
+        own, cross = yb_pair(m, slot)
+        own.start()
+        far = jnp.logical_and(last, m >= RELAY3)
+
+        @pl.when(far)
+        def _():
+            far_send(m, slot).start()
+
+        @pl.when(jnp.logical_not(far))
+        def _():
+            cross.start()
 
     def weight_ops(v):
         grp = v // GROUP
@@ -486,10 +521,18 @@
         f_on = k < N_MB
         p_on = jnp.logical_and(p >= 0, p < N_MB)
         pb_on = jnp.logical_and(b_on, jnp.logical_not(first))
+        w_on = jnp.logical_and(v >= 0, jnp.logical_not(first))
+
+        @pl.when(jnp.logical_and(first, v >= 0))
+        def _():
+            start, run = weight_ops(v)
+            start()
+            run()
 
         @pl.when(b_on)
         def _():
             backward(b, b + jnp.minimum(k, N_MB))
+            relay_back(b + LEAD3)
 
         @pl.when(jnp.logical_and(b_on, p_on))
         def _():
@@ -499,7 +542,7 @@
         def _():
             relay(k - 2)
 
-        @pl.when(v >= 0)
+        @pl.when(w_on)
         def _():
             weight_ops(v)[0]()
 
@@ -519,7 +562,7 @@
         def _():
             backward_post(b)
 
-        @pl.when(v >= 0)
+        @pl.when(w_on)
         def _():
             weight_ops(v)[1]()
 
@@ -556,7 +599,11 @@
 
         @pl.when(st == 1)
         def _():
-            relay_copy(m).wait_send()
+            relay_x(m).wait_send()
+
+        @pl.when(first)
+        def _():
+            relay_e(m).wait_send()
 
     @pl.when(last)
     def _():
@@ -609,25 +656,111 @@
     )(x_in, tgt, w1, w2)
 
 
-def add_tail(acc, left, right, n_row_blk, n_col_blk, name):
-    rows = HB
-
-    def body(acc_ref, l_ref, r_ref, o_ref):
-        o_ref[...] = acc_ref[...] + dot_tn(l_ref[...], r_ref[...])
-
+def tail_kernel(x_all, e_all, a_all, g_all, acc1, acc2, out1, out2, wide, narrow, tile, wide_sem, n_sem, l_sem, s_sem):
+    rows = pl.ds(N_GRP * GTOK, GTOK)
+    n2 = HID // HB
+    n1 = DIM // HB
+
+    def cols(j, width=HB):
+        return pl.ds(pl.multiple_of(j * width, width), width)
+
+    def on_tile(t, fn2, fn1):
+        @pl.when(t < n2)
+        def _():
+            fn2(cols(t))
+
+        @pl.when(t >= n2)
+        def _():
+            fn1(cols(lax.rem(t - n2, n1)), cols((t - n2) // n1, DIM))
+
+    def start_tile(t):
+        slot = lax.rem(t, 4)
+        n_slot = lax.rem(t, 3)
+
+        def fn2(blk):
+            pltpu.make_async_copy(acc2.at[blk, :], tile.at[slot], l_sem.at[slot]).start()
+            pltpu.make_async_copy(a_all.at[rows, blk], narrow.at[n_slot], n_sem.at[n_slot]).start()
+
+        def fn1(dblk, half):
+            pltpu.make_async_copy(acc1.at[dblk, half], tile.at[slot], l_sem.at[slot]).start()
+            pltpu.make_async_copy(x_all.at[rows, dblk], narrow.at[n_slot], n_sem.at[n_slot]).start()
+
+        on_tile(t, fn2, fn1)
+
+    def start_store(t):
+        slot = lax.rem(t, 4)
+
+        def fn2(blk):
+            pltpu.make_async_copy(tile.at[slot], out2.at[blk, :], s_sem.at[slot]).start()
+
+        def fn1(dblk, half):
+            pltpu.make_async_copy(tile.at[slot], out1.at[dblk, half], s_sem.at[slot]).start()
+
+        on_tile(t, fn2, fn1)
+
+    def wait_store(slot):
+        pltpu.make_async_copy(tile.at[slot], out2.at[pl.ds(0, HB), :], s_sem.at[slot]).wait()
+
+    def wide_copy(i):
+        src = e_all.at[rows, :] if i == 0 else g_all.at[rows, pl.ds((i - 1) * DIM, DIM)]
+        return pltpu.make_async_copy(src, wide.at[i], wide_sem.at[i])
+
+    start_tile(0)
+    wide_copy(0).start()
+    start_tile(1)
+
+    @pl.loop(0, n2 + 2 * n1)
+    def _(t):
+        slot = lax.rem(t, 4)
+        n_slot = lax.rem(t, 3)
+
+        @pl.when(t >= 2)
+        def _():
+            wait_store(lax.rem(t + 2, 4))
+
+        @pl.when(t + 2 < n2 + 2 * n1)
+        def _():
+            start_tile(t + 2)
+
+        for i in range(1, 3):
+
+            @pl.when(t == n2 + (i - 1) * n1 - 4)
+            def _():
+                wide_copy(i).start()
+
+        for i in range(3):
+
+            @pl.when(t == (0 if i == 0 else n2 + (i - 1) * n1))
+            def _():
+                wide_copy(i).wait()
+
+        pltpu.make_async_copy(a_all.at[rows, pl.ds(0, HB)], narrow.at[n_slot], n_sem.at[n_slot]).wait()
+        pltpu.make_async_copy(acc2.at[pl.ds(0, HB), :], tile.at[slot], l_sem.at[slot]).wait()
+        which = jnp.where(t < n2, 0, 1 + (t - n2) // n1)
+        tile[slot] += dot_tn(narrow[n_slot], wide[which])
+        start_store(t)
+
+    wait_store(2)
+    wait_store(3)
+
+
+def add_tail(x_all, e_all, a_all, g_all, acc1, acc2):
+    hbm = pl.BlockSpec(memory_space=pl.ANY)
+    dma = pltpu.SemaphoreType.DMA
     return pl.pallas_call(
-        body,
-        grid=(n_col_blk, n_row_blk),
-        in_specs=[
-            pl.BlockSpec((rows, DIM), lambda c, r: (r, c)),
-            pl.BlockSpec((GTOK, rows), lambda c, r: (N_GRP, r)),
-            pl.BlockSpec((GTOK, DIM), lambda c, r: (N_GRP, c)),
+        tail_kernel,
+        in_specs=[hbm] * 6,
+        out_specs=[hbm] * 2,
+        out_shape=[jax.ShapeDtypeStruct(acc1.shape, F32), jax.ShapeDtypeStruct(acc2.shape, F32)],
+        scratch_shapes=[
+            pltpu.VMEM((3, GTOK, DIM), BF),
+            pltpu.VMEM((3, GTOK, HB), BF),
+            pltpu.VMEM((4, HB, DIM), F32),
+            dma((3,)), dma((3,)), dma((4,)), dma((4,)),
         ],
-        out_specs=pl.BlockSpec((rows, DIM), lambda c, r: (r, c)),
-        out_shape=jax.ShapeDtypeStruct(acc.shape, F32),
-        compiler_params=pltpu.CompilerParams(vmem_limit_bytes=56_000_000),
-        name=name,
-    )(acc, left, right)
+        compiler_params=pltpu.CompilerParams(vmem_limit_bytes=60_000_000),
+        name="tail",
+    )(x_all, e_all, a_all, g_all, acc1, acc2)
 
 
 def solution(mesh):
@@ -636,8 +769,7 @@
         x_in = inputs.reshape(tokens, DIM)
         tgt = targets.reshape(tokens, DIM)
         x_all, e_all, _, a_all, g_all, _, _, _, acc1, acc2, loss = run_pipeline(x_in, tgt, w_in[0, 0], w_out[0, 0])
-        grad_in = add_tail(acc1, x_all, g_all, DIM // HB, HID // DIM, "tail_in")
-        grad_out = add_tail(acc2, a_all, e_all, HID // HB, 1, "tail_out")
+        grad_in, grad_out = add_tail(x_all, e_all, a_all, g_all, acc1, acc2)
         total = jnp.sum(loss) * (0.5 / N_ELEM)
         return grad_in[None, None], grad_out[None, None], jnp.reshape(total, (1,))
 

time: 2390 us -> 2360 us (0.987)
  Pallas kernels: 2390 us -> 2350 us
    pallas_call x2 -> x1, Pallas kernels: 100 us -> 82.6 us  [add_tail(): pl.pallas_call(tail_kernel, in_specs=[hbm] * 6, out_specs=[hbm] * 2, out_...]
where the time goes in v4:
time: 2360 us; the launch traced here: 2350 us
  Pallas kernels  2350 us (100%)
    pallas_call x1, Pallas kernels, run_pipeline(): pl.pallas_call(pipeline_kernel, out_shape=out_shape, in_specs=[hbm] * 4,...  2270 us
    pallas_call x1, Pallas kernels, add_tail(): pl.pallas_call(tail_kernel, in_specs=[hbm] * 6, out_specs=[hbm] * 2, out_...  82.6 us

profile of v4, /device:TPU:0, one launch (start us, length us, event | category | flops | bytes accessed | tf_op | source)
XLA Modules:
  0.0 2351.4 jit_solution(16512399136835475318)
XLA Ops:
  0.6 2265.1 %pipeline.1 = (bf16[6144,2560]{1,0:T(8,128)(2,1)}, bf16[6144,2560]{1,0:T(8,128)(2,1)}, bf16[6144,5120]{1,0:T(8,128)(2,1)}, bf16[6144,5120]{1,0:T(8,128)(2,1)}, b...) custom-call(bf16[6144,2560]{1,0:T(8,128)(2,1)} %bitcast.7, ...), custom_call_target="tpu_custom_call" | custom-call | tf_op jit(solution)/shard_map/pipeline/pallas_call | solution.py:625
  2265.7 1.3 reduce_sum.9
  2267.7 82.6 %tail.1 = (f32[2560,5120]{1,0:T(8,128)}, f32[5120,2560]{1,0:T(8,128)}) custom-call(bf16[6144,2560]{1,0:T(8,128)(2,1)} %get-tuple-element.12.x_all, bf16[6144,2560]{1,0:T(8,128)(2,1)} %get-tuple-element.13.e_all, bf16[6144,5120]{1,0:T(8,128)(2,1)} %get-tuple-element.14.a_all, bf16[6144,5120]{1,0:T(8,128)(2,1)} %get-tuple-element.15.g_all, ...), custom_call_target="tpu_custom_call" | custom-call | tf_op jit(solution)/shard_map/tail/pallas_call | solution.py:750

commit v5 on v4

--- a/solution.py
+++ b/solution.py
@@ -16,6 +16,8 @@
 HB = 512
 N_BLK = HID // HB
 W_SLOTS = 3
+WT = HB // 2
+N_WT = 6
 GROUP = 4
 N_GRP = N_MB // GROUP - 1
 GTOK = GROUP * TOK
@@ -52,7 +54,7 @@
 def pipeline_kernel(
     x_in, tgt, w1, w2,
     x_all, e_all, u_all, a_all, g_all, rsf, rsb, fwd, acc1, acc2, loss,
-    xbuf, w1buf, w2buf, ubuf, abuf, gbuf, uin, accf, accb, rsv, res, tbuf, yf, yb, wide, narrow, wtile, lsum, lrx,
+    xbuf, w1buf, w2buf, ubuf0, ubuf1, abuf0, abuf1, gbuf0, gbuf1, uin0, uin1, qbuf, accf, accb, rsv, res, tbuf, yf, yb, wide, narrow, wtile, lsum, lrx,
     w_sem, x_sem, uo_sem, ao_sem, go_sem, ui_sem, p_sem, wd_sem, wn_sem, wl_sem, ws_sem,
     xr_sem, er_sem, rf_sem, rb_sem, sf_sem, sb_sem, yf_sem, yb_sem, fr_sem, fs_sem, ls_sem, lr_sem,
 ):
@@ -78,11 +80,20 @@
     def cols(j, width=HB):
         return pl.ds(pl.multiple_of(j * width, width), width)
 
-    def w_copies(j, slot):
-        return (
-            pltpu.make_async_copy(w1.at[:, cols(j)], w1buf.at[slot], w_sem.at[slot, 0]),
-            pltpu.make_async_copy(w2.at[cols(j), :], w2buf.at[slot], w_sem.at[slot, 1]),
-        )
+    ubuf, abuf, gbuf, uin = (ubuf0, ubuf1), (abuf0, abuf1), (gbuf0, gbuf1), (uin0, uin1)
+
+    def w1_copy(j, slot):
+        return pltpu.make_async_copy(w1.at[:, cols(j)], w1buf.at[slot], w_sem.at[slot, 0])
+
+    def w2_copy(j, slot):
+        return pltpu.make_async_copy(w2.at[cols(j), :], w2buf.at[slot], w_sem.at[slot, 1])
+
+    def use(copy, at):
+        slot = lax.rem(at, W_SLOTS)
+        copy(lax.rem(at, N_BLK), slot).wait()
+        ahead = at + W_SLOTS - 1
+        copy(lax.rem(ahead, N_BLK), lax.rem(ahead, W_SLOTS)).start()
+        return slot
 
     def rs_copy(acc, slot, buf, m, send, recv):
         return pltpu.make_async_remote_copy(
@@ -167,28 +178,21 @@
             pltpu.make_async_copy(ref, ref, recv.at[m, half]).wait()
 
     def out_copy(buf, slot, dst, m, j, sem):
-        return pltpu.make_async_copy(buf.at[slot], dst.at[mb_rows(m), cols(j)], sem.at[slot])
+        return pltpu.make_async_copy(buf[slot], dst.at[mb_rows(m), cols(j)], sem.at[slot])
 
     def u_load(m, j, slot):
-        return pltpu.make_async_copy(u_all.at[mb_rows(m), cols(j)], uin.at[slot], ui_sem.at[slot])
-
-    def load_x(src, m):
+        return pltpu.make_async_copy(u_all.at[mb_rows(m), cols(j)], uin[slot], ui_sem.at[slot])
+
+    def load_x(src, m, also=None):
         cp = pltpu.make_async_copy(src.at[mb_rows(m), :], xbuf, x_sem)
         cp.start()
+        if also is not None:
+            also()
         cp.wait()
 
-    def next_weights(count, j):
-        at = count * N_BLK + j
-        slot = lax.rem(at, W_SLOTS)
-        for cp in w_copies(j, slot):
-            cp.wait()
-        ahead = W_SLOTS - 1
-        for cp in w_copies(lax.rem(j + ahead, N_BLK), lax.rem(at + ahead, W_SLOTS)):
-            cp.start()
-        return slot
-
-    def forward(m, count):
+    def forward(m, count, also):
         slot_m = lax.rem(m, 2)
+        base = count * N_BLK
 
         @pl.when(first)
         def _():
@@ -203,33 +207,43 @@
         @pl.when(jnp.logical_not(first))
         def _():
             wait_in(x_all, m, xr_sem)
-            load_x(x_all, m)
+            load_x(x_all, m, also)
 
         @pl.when(m >= 2)
         def _():
             rs_copy(accf, slot_m, rsf, m - 2, sf_sem, rf_sem).wait_send()
 
-        @pl.loop(0, N_BLK)
-        def _(j):
-            slot = lax.rem(j, 2)
-            ws = next_weights(count, j)
-
-            @pl.when(m * N_BLK + j >= 2)
-            def _():
+        def block(j, slot):
+            w1s = use(w1_copy, base + j)
+            w2s = None if isinstance(j, int) and j == 0 else use(w2_copy, base + j - 1)
+
+            def drain():
                 out_copy(ubuf, slot, u_all, m, j, uo_sem).wait()
                 out_copy(abuf, slot, a_all, m, j, ao_sem).wait()
 
-            ubuf[slot] = dot_nn(xbuf[...], w1buf[ws]).astype(BF)
-            abuf[slot] = gelu(ubuf[slot].astype(F32)).astype(BF)
+            if isinstance(j, int) and j == 0:
+                pl.when(m >= 1)(drain)
+            else:
+                pl.when(jnp.logical_or(m >= 1, j >= 2))(drain)
+            ubuf[slot][...] = dot_nn(xbuf[...], w1buf[w1s]).astype(BF)
+            if w2s is None:
+                accf[slot_m] = jnp.zeros((TOK, DIM), F32)
+            else:
+                accf[slot_m] += dot_nn(abuf[1 - slot][...], w2buf[w2s])
+            abuf[slot][...] = gelu(ubuf[slot][...].astype(F32)).astype(BF)
             out_copy(ubuf, slot, u_all, m, j, uo_sem).start()
             out_copy(abuf, slot, a_all, m, j, ao_sem).start()
 
-            @pl.when(j == 0)
-            def _():
-                accf[slot_m] = jnp.zeros((TOK, DIM), F32)
-
-            accf[slot_m] += dot_nn(abuf[slot], w2buf[ws])
-
+        block(0, 0)
+
+        @pl.loop(0, (N_BLK - 2) // 2)
+        def _(i):
+            block(2 * i + 1, 1)
+            block(2 * i + 2, 0)
+
+        block(N_BLK - 1, 1)
+        w2s = use(w2_copy, base + N_BLK - 1)
+        accf[slot_m] += dot_nn(abuf[1][...], w2buf[w2s])
         rs_copy(accf, slot_m, rsf, m, sf_sem, rf_sem).start()
 
         @pl.when(m == N_MB - 1)
@@ -346,6 +360,7 @@
 
     def backward(m, count):
         slot_m = lax.rem(m, 2)
+        base = count * N_BLK
         u_load(m, 0, 0).start()
         wait_in(e_all, m, er_sem)
         load_x(e_all, m)
@@ -354,35 +369,47 @@
         def _():
             rs_copy(accb, slot_m, rsb, m - 2, sb_sem, rb_sem).wait_send()
 
-        @pl.loop(0, N_BLK)
-        def _(j):
-            slot = lax.rem(j, 2)
-            ws = next_weights(count, j)
+        def block(j, slot, chain):
+            start = isinstance(j, int) and j == 0
+            w2s = use(w2_copy, base + j)
+            w1s = None if start else use(w1_copy, base + j - 1)
             u_load(m, j, slot).wait()
-
-            @pl.when(j + 1 < N_BLK)
-            def _():
+            if not (isinstance(j, int) and j == N_BLK - 1):
                 u_load(m, j + 1, 1 - slot).start()
-
-            @pl.when(m * N_BLK + j >= 2)
-            def _():
-                out_copy(gbuf, slot, g_all, m, j, go_sem).wait()
-
-            q = dot_nt(xbuf[...], w2buf[ws]).astype(BF)
-            gbuf[slot] = (gelu_slope(uin[slot].astype(F32)) * q.astype(F32)).astype(BF)
+            drain = out_copy(gbuf, slot, g_all, m, j, go_sem).wait
+            if start:
+                pl.when(m >= 1)(drain)
+            else:
+                pl.when(jnp.logical_or(m >= 1, j >= 2))(drain)
+            qbuf[...] = dot_nt(xbuf[...], w2buf[w2s]).astype(BF)
+            if chain and start:
+                accb[slot_m] = jnp.zeros((TOK, DIM), F32)
+            elif chain:
+                accb[slot_m] += dot_nt(gbuf[1 - slot][...], w1buf[w1s])
+            gbuf[slot][...] = (gelu_slope(uin[slot][...].astype(F32)) * qbuf[...].astype(F32)).astype(BF)
             out_copy(gbuf, slot, g_all, m, j, go_sem).start()
 
-            @pl.when(jnp.logical_not(first))
-            def _():
-                @pl.when(j == 0)
-                def _():
-                    accb[slot_m] = jnp.zeros((TOK, DIM), F32)
-
-                accb[slot_m] += dot_nt(gbuf[slot], w1buf[ws])
+        def blocks(chain):
+            block(0, 0, chain)
+
+            @pl.loop(0, (N_BLK - 2) // 2)
+            def _(i):
+                block(2 * i + 1, 1, chain)
+                block(2 * i + 2, 0, chain)
+
+            block(N_BLK - 1, 1, chain)
+            w1s = use(w1_copy, base + N_BLK - 1)
+            if chain:
+                accb[slot_m] += dot_nt(gbuf[1][...], w1buf[w1s])
+                rs_copy(accb, slot_m, rsb, m, sb_sem, rb_sem).start()
+
+        @pl.when(first)
+        def _():
+            blocks(False)
 
         @pl.when(jnp.logical_not(first))
         def _():
-            rs_copy(accb, slot_m, rsb, m, sb_sem, rb_sem).start()
+            blocks(True)
 
     def backward_post(m):
         slot = lax.rem(m, 2)
@@ -416,15 +443,15 @@
         def on_tile(t, fn2, fn1):
             @pl.when(out2)
             def _():
-                fn2(cols(quart * 5 + t))
+                fn2(cols(quart * (HID // WT // 2) + t, WT))
 
             @pl.when(jnp.logical_not(out2))
             def _():
-                fn1(cols(t), cols(quart - 2, DIM))
+                fn1(cols(t, WT), cols(quart - 2, DIM))
 
         def start_tile(t):
-            n_slot = lax.rem(t, 2)
-            slot = lax.rem(t, 3)
+            n_slot = lax.rem(t, 4)
+            slot = lax.rem(t, N_WT)
 
             def fn2(blk):
                 pltpu.make_async_copy(a_all.at[rows, blk], narrow.at[n_slot], wn_sem.at[n_slot]).start()
@@ -449,7 +476,7 @@
             on_tile(t, fn2, fn1)
 
         def start_store(t):
-            slot = lax.rem(t, 3)
+            slot = lax.rem(t, N_WT)
 
             def fn2(blk):
                 pltpu.make_async_copy(wtile.at[slot], acc2.at[blk, :], ws_sem.at[slot]).start()
@@ -460,7 +487,7 @@
             on_tile(t, fn2, fn1)
 
         def wait_store(slot):
-            pltpu.make_async_copy(wtile.at[slot], acc2.at[pl.ds(0, HB), :], ws_sem.at[slot]).wait()
+            pltpu.make_async_copy(wtile.at[slot], acc2.at[pl.ds(0, WT), :], ws_sem.at[slot]).wait()
 
         def start():
             @pl.when(out2)
@@ -471,46 +498,51 @@
             def _():
                 pltpu.make_async_copy(g_all.at[rows, cols(quart - 2, DIM)], wide, wd_sem).start()
 
-            start_tile(0)
-
-        def run():
-            pltpu.make_async_copy(e_all.at[rows, :], wide, wd_sem).wait()
-
-            @pl.loop(0, 5)
+            for t in range(N_WT // 2):
+                start_tile(t)
+
+        n_tiles = DIM // WT
+
+        def run(low, high):
+            if low == 0:
+                pltpu.make_async_copy(e_all.at[rows, :], wide, wd_sem).wait()
+
+            @pl.loop(low, high)
             def _(t):
-                slot = lax.rem(t, 3)
-                n_slot = lax.rem(t, 2)
-
-                @pl.when(t >= 2)
+                slot = lax.rem(t, N_WT)
+                n_slot = lax.rem(t, 4)
+
+                @pl.when(t >= N_WT // 2)
                 def _():
-                    wait_store(lax.rem(t + 1, 3))
-
-                @pl.when(t < 4)
+                    wait_store(lax.rem(t + N_WT // 2, N_WT))
+
+                @pl.when(t + N_WT // 2 < n_tiles)
                 def _():
-                    start_tile(t + 1)
-
-                pltpu.make_async_copy(a_all.at[rows, pl.ds(0, HB)], narrow.at[n_slot], wn_sem.at[n_slot]).wait()
+                    start_tile(t + N_WT // 2)
+
+                pltpu.make_async_copy(a_all.at[rows, pl.ds(0, WT)], narrow.at[n_slot], wn_sem.at[n_slot]).wait()
 
                 @pl.when(grp > 0)
                 def _():
-                    pltpu.make_async_copy(acc2.at[pl.ds(0, HB), :], wtile.at[slot], wl_sem.at[slot]).wait()
+                    pltpu.make_async_copy(acc2.at[pl.ds(0, WT), :], wtile.at[slot], wl_sem.at[slot]).wait()
 
                 @pl.when(grp == 0)
                 def _():
-                    wtile[slot] = jnp.zeros((HB, DIM), F32)
+                    wtile[slot] = jnp.zeros((WT, DIM), F32)
 
                 wtile[slot] += dot_tn(narrow[n_slot], wide[...])
                 start_store(t)
 
-            wait_store(0)
-            wait_store(1)
+            if high == n_tiles:
+                for t in range(n_tiles - N_WT // 2, n_tiles):
+                    wait_store(t % N_WT)
 
         return start, run
 
     lsum[...] = jnp.zeros((8, 128), F32)
     for j in range(W_SLOTS - 1):
-        for cp in w_copies(j, j):
-            cp.start()
+        w1_copy(j, j).start()
+        w2_copy(j, j).start()
 
     @pl.loop(0, N_MB + warm)
     def _(k):
@@ -527,7 +559,7 @@
         def _():
             start, run = weight_ops(v)
             start()
-            run()
+            run(0, DIM // WT)
 
         @pl.when(b_on)
         def _():
@@ -542,41 +574,47 @@
         def _():
             relay(k - 2)
 
+        @pl.when(jnp.logical_and(w_on, jnp.logical_not(f_on)))
+        def _():
+            weight_ops(v)[0]()
+
+        @pl.when(f_on)
+        def _():
+            forward(k, k + jnp.maximum(b + 1, 0), lambda: pl.when(w_on)(weight_ops(v)[0]))
+
+        @pl.when(jnp.logical_and(jnp.logical_not(b_on), p_on))
+        def _():
+            forward_post(p)
+
+        @pl.when(jnp.logical_not(b_on))
+        def _():
+            relay(k - 2)
+
+        @pl.when(jnp.logical_and(pb_on, f_on))
+        def _():
+            backward_post(b)
+
+        half_tiles = DIM // WT // 2
+
         @pl.when(w_on)
         def _():
-            weight_ops(v)[0]()
-
-        @pl.when(f_on)
-        def _():
-            forward(k, k + jnp.maximum(b + 1, 0))
-
-        @pl.when(jnp.logical_and(jnp.logical_not(b_on), p_on))
-        def _():
-            forward_post(p)
-
-        @pl.when(jnp.logical_not(b_on))
-        def _():
-            relay(k - 2)
-
-        @pl.when(jnp.logical_and(pb_on, f_on))
+            weight_ops(v)[1](0, half_tiles)
+
+        @pl.when(jnp.logical_and(pb_on, jnp.logical_not(f_on)))
         def _():
             backward_post(b)
 
         @pl.when(w_on)
         def _():
-            weight_ops(v)[1]()
-
-        @pl.when(jnp.logical_and(pb_on, jnp.logical_not(f_on)))
-        def _():
-            backward_post(b)
+            weight_ops(v)[1](half_tiles, 2 * half_tiles)
 
     for half in range(2):
         pltpu.make_async_copy(lsum, lrx.at[half], lr_sem.at[half]).wait()
     loss[...] = lrx[0] + lrx[1]
 
     for j in range(W_SLOTS - 1):
-        for cp in w_copies(j, (2 * N_MB * N_BLK + j) % W_SLOTS):
-            cp.wait()
+        w1_copy(j, (2 * N_MB * N_BLK + j) % W_SLOTS).wait()
+        w2_copy(j, (2 * N_MB * N_BLK + j) % W_SLOTS).wait()
     for m in (N_MB - 2, N_MB - 1):
         slot = m % 2
         out_copy(gbuf, slot, g_all, m, 0, go_sem).wait()
@@ -631,10 +669,11 @@
             pltpu.VMEM((TOK, DIM), BF),
             pltpu.VMEM((W_SLOTS, DIM, HB), BF),
             pltpu.VMEM((W_SLOTS, HB, DIM), BF),
-            pltpu.VMEM((2, TOK, HB), BF),
-            pltpu.VMEM((2, TOK, HB), BF),
-            pltpu.VMEM((2, TOK, HB), BF),
-            pltpu.VMEM((2, TOK, HB), BF),
+            pltpu.VMEM((TOK, HB), BF), pltpu.VMEM((TOK, HB), BF),
+            pltpu.VMEM((TOK, HB), BF), pltpu.VMEM((TOK, HB), BF),
+            pltpu.VMEM((TOK, HB), BF), pltpu.VMEM((TOK, HB), BF),
+            pltpu.VMEM((TOK, HB), BF), pltpu.VMEM((TOK, HB), BF),
+            pltpu.VMEM((TOK, HB), BF),
             pltpu.VMEM((2, TOK, DIM), F32),
             pltpu.VMEM((2, TOK, DIM), F32),
             pltpu.VMEM((HALF, DIM), F32),
@@ -643,11 +682,11 @@
             pltpu.VMEM((2, HALF, DIM), BF),
             pltpu.VMEM((2, HALF, DIM), BF),
             pltpu.VMEM((GTOK, DIM), BF),
-            pltpu.VMEM((2, GTOK, HB), BF),
-            pltpu.VMEM((3, HB, DIM), F32),
+            pltpu.VMEM((4, GTOK, WT), BF),
+            pltpu.VMEM((N_WT, WT, DIM), F32),
             pltpu.VMEM((8, 128), F32),
             pltpu.VMEM((2, 8, 128), F32),
-            dma((W_SLOTS, 2)), dma, dma((2,)), dma((2,)), dma((2,)), dma((2,)), dma((3,)), dma, dma((2,)), dma((3,)), dma((3,)),
+            dma((W_SLOTS, 2)), dma, dma((2,)), dma((2,)), dma((2,)), dma((2,)), dma((3,)), dma, dma((4,)), dma((N_WT,)), dma((N_WT,)),
             dma((N_MB, 2)), dma((N_MB, 2)), dma((N_MB,)), dma((N_MB,)), dma((2,)), dma((2,)), dma((2, 2)), dma((2, 2)),
             dma((N_MB,)), dma((2,)), dma((8,)), dma((2,)),
         ],

time: 2360 us -> 2230 us (0.945)
  Pallas kernels: 2350 us -> 2220 us
    pallas_call x1, Pallas kernels: 2270 us -> 2140 us  [run_pipeline(): pl.pallas_call(pipeline_kernel, out_shape=out_shape, in_specs=[hbm] * 4,...]
where the time goes in v5:
time: 2230 us
  Pallas kernels  2220 us (100%)
    pallas_call x1, Pallas kernels, run_pipeline(): pl.pallas_call(pipeline_kernel, out_shape=out_shape, in_specs=[hbm] * 4,...  2140 us
    pallas_call x1, Pallas kernels, add_tail(): pl.pallas_call(tail_kernel, in_specs=[hbm] * 6, out_specs=[hbm] * 2, out_...  82.6 us

profile of v5, /device:TPU:0, one launch (start us, length us, event | category | flops | bytes accessed | tf_op | source)
XLA Modules:
  0.0 2227.0 jit_solution(15226980374711427089)
XLA Ops:
  0.6 2140.7 %pipeline.1 = (bf16[6144,2560]{1,0:T(8,128)(2,1)}, bf16[6144,2560]{1,0:T(8,128)(2,1)}, bf16[6144,5120]{1,0:T(8,128)(2,1)}, bf16[6144,5120]{1,0:T(8,128)(2,1)}, b...) custom-call(bf16[6144,2560]{1,0:T(8,128)(2,1)} %bitcast.7, ...), custom_call_target="tpu_custom_call" | custom-call | tf_op jit(solution)/shard_map/pipeline/pallas_call | solution.py:663
  2141.3 1.3 reduce_sum.9
  2143.3 82.6 %tail.1 = (f32[2560,5120]{1,0:T(8,128)}, f32[5120,2560]{1,0:T(8,128)}) custom-call(bf16[6144,2560]{1,0:T(8,128)(2,1)} %get-tuple-element.12.x_all, bf16[6144,2560]{1,0:T(8,128)(2,1)} %get-tuple-element.13.e_all, bf16[6144,5120]{1,0:T(8,128)(2,1)} %get-tuple-element.14.a_all, bf16[6144,5120]{1,0:T(8,128)(2,1)} %get-tuple-element.15.g_all, ...), custom_call_target="tpu_custom_call" | custom-call | tf_op jit(solution)/shard_map/tail/pallas_call | solution.py:789

commit v6 on v5

--- a/solution.py
+++ b/solution.py
@@ -23,7 +23,7 @@
 GTOK = GROUP * TOK
 N_ELEM = N_MB * TOK * DIM
 RELAY0 = 3
-RELAY3 = 10
+RELAY3 = 6
 LEAD3 = 3
 MESH = pl.DeviceIdType.MESH
 BF = jnp.bfloat16
@@ -54,8 +54,8 @@
 def pipeline_kernel(
     x_in, tgt, w1, w2,
     x_all, e_all, u_all, a_all, g_all, rsf, rsb, fwd, acc1, acc2, loss,
-    xbuf, w1buf, w2buf, ubuf0, ubuf1, abuf0, abuf1, gbuf0, gbuf1, uin0, uin1, qbuf, accf, accb, rsv, res, tbuf, yf, yb, wide, narrow, wtile, lsum, lrx,
-    w_sem, x_sem, uo_sem, ao_sem, go_sem, ui_sem, p_sem, wd_sem, wn_sem, wl_sem, ws_sem,
+    xbuf, tall, flat, ubuf0, ubuf1, uin0, uin1, qbuf0, qbuf1, mid, accf, accb, rsv, res, tbuf, yf, yb, wide, narrow, wtile, lsum, lrx,
+    t_sem, f_sem, x_sem, uo_sem, m_sem, ui_sem, p_sem, wd_sem, wn_sem, wl_sem, ws_sem,
     xr_sem, er_sem, rf_sem, rb_sem, sf_sem, sb_sem, yf_sem, yb_sem, fr_sem, fs_sem, ls_sem, lr_sem,
 ):
     my = lax.axis_index("model")
@@ -63,7 +63,7 @@
     other = 1 - my
     last = st == 3
     first = st == 0
-    warm = jnp.where(st == 0, 16, jnp.where(st == 1, 10, jnp.where(st == 2, 5, 2)))
+    warm = jnp.where(st == 0, 16, jnp.where(st == 1, 9, jnp.where(st == 2, 5, 2)))
     partner = {"model": other}
     nxt = jnp.minimum(st + 1, 3)
     prv = jnp.maximum(st - 1, 0)
@@ -80,19 +80,45 @@
     def cols(j, width=HB):
         return pl.ds(pl.multiple_of(j * width, width), width)
 
-    ubuf, abuf, gbuf, uin = (ubuf0, ubuf1), (abuf0, abuf1), (gbuf0, gbuf1), (uin0, uin1)
-
-    def w1_copy(j, slot):
-        return pltpu.make_async_copy(w1.at[:, cols(j)], w1buf.at[slot], w_sem.at[slot, 0])
-
-    def w2_copy(j, slot):
-        return pltpu.make_async_copy(w2.at[cols(j), :], w2buf.at[slot], w_sem.at[slot, 1])
-
-    def use(copy, at):
+    ubuf, uin, qbuf = (ubuf0, ubuf1), (uin0, uin1), (qbuf0, qbuf1)
+    n_back = jnp.where(first, N_BLK, 2 * N_BLK)
+
+    def tall_start(at):
         slot = lax.rem(at, W_SLOTS)
-        copy(lax.rem(at, N_BLK), slot).wait()
-        ahead = at + W_SLOTS - 1
-        copy(lax.rem(ahead, N_BLK), lax.rem(ahead, W_SLOTS)).start()
+        j = lax.rem(at, 2 * N_BLK)
+        i = jnp.maximum(j - N_BLK, 0)
+
+        @pl.when(j < N_BLK)
+        def _():
+            pltpu.make_async_copy(w1.at[:, cols(j)], tall.at[slot], t_sem.at[slot]).start()
+
+        @pl.when(j >= N_BLK)
+        def _():
+            pltpu.make_async_copy(w2.at[cols(lax.rem(i, 2), DIM), cols(i // 2)], tall.at[slot], t_sem.at[slot]).start()
+
+    def tall_wait(slot):
+        pltpu.make_async_copy(w1.at[:, cols(0)], tall.at[slot], t_sem.at[slot]).wait()
+
+    def flat_start(at):
+        slot = lax.rem(at, W_SLOTS)
+        j = lax.rem(at, n_back)
+        i = jnp.maximum(j - N_BLK, 0)
+
+        @pl.when(j < N_BLK)
+        def _():
+            pltpu.make_async_copy(w2.at[cols(j), :], flat.at[slot], f_sem.at[slot]).start()
+
+        @pl.when(j >= N_BLK)
+        def _():
+            pltpu.make_async_copy(w1.at[cols(i // 2), cols(lax.rem(i, 2), DIM)], flat.at[slot], f_sem.at[slot]).start()
+
+    def flat_wait(slot):
+        pltpu.make_async_copy(w2.at[cols(0), :], flat.at[slot], f_sem.at[slot]).wait()
+
+    def use(start, wait, at):
+        slot = lax.rem(at, W_SLOTS)
+        wait(slot)
+        start(at + W_SLOTS - 1)
         return slot
 
     def rs_copy(acc, slot, buf, m, send, recv):
@@ -105,6 +131,16 @@
             device_id_type=MESH,
         )
 
+    def rs_part(acc, slot, buf, m, c, send, recv):
+        return pltpu.make_async_remote_copy(
+            src_ref=acc.at[slot, half_rows(other), cols(c)],
+            dst_ref=buf.at[pl.ds(pl.multiple_of(m * HALF, HALF), HALF), cols(c)],
+            send_sem=send.at[slot],
+            recv_sem=recv.at[m],
+            device_id=partner,
+            device_id_type=MESH,
+        )
+
     def half_copy(src, slot, dst, m, half, send, k, recv, dev):
         return pltpu.make_async_remote_copy(
             src_ref=src.at[slot],
@@ -180,6 +216,9 @@
     def out_copy(buf, slot, dst, m, j, sem):
         return pltpu.make_async_copy(buf[slot], dst.at[mb_rows(m), cols(j)], sem.at[slot])
 
+    def mid_copy(dst, m):
+        return pltpu.make_async_copy(mid, dst.at[mb_rows(m), :], m_sem)
+
     def u_load(m, j, slot):
         return pltpu.make_async_copy(u_all.at[mb_rows(m), cols(j)], uin[slot], ui_sem.at[slot])
 
@@ -190,9 +229,9 @@
             also()
         cp.wait()
 
-    def forward(m, count, also):
+    def forward(m, also):
         slot_m = lax.rem(m, 2)
-        base = count * N_BLK
+        base = m * 2 * N_BLK
 
         @pl.when(first)
         def _():
@@ -213,26 +252,20 @@
         def _():
             rs_copy(accf, slot_m, rsf, m - 2, sf_sem, rf_sem).wait_send()
 
+        def activate(j, slot):
+            mid[:, cols(j)] = gelu(ubuf[slot][...].astype(F32)).astype(BF)
+
         def block(j, slot):
-            w1s = use(w1_copy, base + j)
-            w2s = None if isinstance(j, int) and j == 0 else use(w2_copy, base + j - 1)
-
-            def drain():
+            ws = use(tall_start, tall_wait, base + j)
+
+            @pl.when(j >= 2)
+            def _():
                 out_copy(ubuf, slot, u_all, m, j, uo_sem).wait()
-                out_copy(abuf, slot, a_all, m, j, ao_sem).wait()
-
-            if isinstance(j, int) and j == 0:
-                pl.when(m >= 1)(drain)
-            else:
-                pl.when(jnp.logical_or(m >= 1, j >= 2))(drain)
-            ubuf[slot][...] = dot_nn(xbuf[...], w1buf[w1s]).astype(BF)
-            if w2s is None:
-                accf[slot_m] = jnp.zeros((TOK, DIM), F32)
-            else:
-                accf[slot_m] += dot_nn(abuf[1 - slot][...], w2buf[w2s])
-            abuf[slot][...] = gelu(ubuf[slot][...].astype(F32)).astype(BF)
+
+            ubuf[slot][...] = dot_nn(xbuf[...], tall[ws]).astype(BF)
+            if not (isinstance(j, int) and j == 0):
+                activate(j - 1, 1 - slot)
             out_copy(ubuf, slot, u_all, m, j, uo_sem).start()
-            out_copy(abuf, slot, a_all, m, j, ao_sem).start()
 
         block(0, 0)
 
@@ -242,15 +275,20 @@
             block(2 * i + 2, 0)
 
         block(N_BLK - 1, 1)
-        w2s = use(w2_copy, base + N_BLK - 1)
-        accf[slot_m] += dot_nn(abuf[1][...], w2buf[w2s])
-        rs_copy(accf, slot_m, rsf, m, sf_sem, rf_sem).start()
-
-        @pl.when(m == N_MB - 1)
-        def _():
-            for slot in range(2):
-                out_copy(ubuf, slot, u_all, m, slot, uo_sem).wait()
-                out_copy(abuf, slot, a_all, m, slot, ao_sem).wait()
+        activate(N_BLK - 1, 1)
+        mid_copy(a_all, m).start()
+
+        @pl.loop(0, DIM // HB)
+        def _(c):
+            ws = use(tall_start, tall_wait, base + N_BLK + 2 * c)
+            accf[slot_m, :, cols(c)] = dot_nn(mid[:, 0:DIM], tall[ws])
+            ws = use(tall_start, tall_wait, base + N_BLK + 2 * c + 1)
+            accf[slot_m, :, cols(c)] += dot_nn(mid[:, DIM:HID], tall[ws])
+            rs_part(accf, slot_m, rsf, m, c, sf_sem, rf_sem).start()
+
+        for slot in range(2):
+            out_copy(ubuf, slot, u_all, m, slot, uo_sem).wait()
+        mid_copy(a_all, m).wait()
 
     def load_post(acc_buf, m, recv, src):
         ref = acc_buf.at[pl.ds(pl.multiple_of(m * HALF, HALF), HALF), :]
@@ -358,10 +396,9 @@
                 )
                 yield (True if s < 3 else my != y), cp
 
-    def backward(m, count):
+    def backward(m):
         slot_m = lax.rem(m, 2)
-        base = count * N_BLK
-        u_load(m, 0, 0).start()
+        base = m * n_back
         wait_in(e_all, m, er_sem)
         load_x(e_all, m)
 
@@ -369,47 +406,42 @@
         def _():
             rs_copy(accb, slot_m, rsb, m - 2, sb_sem, rb_sem).wait_send()
 
-        def block(j, slot, chain):
+        def slope(j, slot):
+            mid[:, cols(j)] = (gelu_slope(uin[slot][...].astype(F32)) * qbuf[slot][...].astype(F32)).astype(BF)
+
+        def block(j, slot):
             start = isinstance(j, int) and j == 0
-            w2s = use(w2_copy, base + j)
-            w1s = None if start else use(w1_copy, base + j - 1)
-            u_load(m, j, slot).wait()
-            if not (isinstance(j, int) and j == N_BLK - 1):
-                u_load(m, j + 1, 1 - slot).start()
-            drain = out_copy(gbuf, slot, g_all, m, j, go_sem).wait
-            if start:
-                pl.when(m >= 1)(drain)
-            else:
-                pl.when(jnp.logical_or(m >= 1, j >= 2))(drain)
-            qbuf[...] = dot_nt(xbuf[...], w2buf[w2s]).astype(BF)
-            if chain and start:
-                accb[slot_m] = jnp.zeros((TOK, DIM), F32)
-            elif chain:
-                accb[slot_m] += dot_nt(gbuf[1 - slot][...], w1buf[w1s])
-            gbuf[slot][...] = (gelu_slope(uin[slot][...].astype(F32)) * qbuf[...].astype(F32)).astype(BF)
-            out_copy(gbuf, slot, g_all, m, j, go_sem).start()
-
-        def blocks(chain):
-            block(0, 0, chain)
-
-            @pl.loop(0, (N_BLK - 2) // 2)
-            def _(i):
-                block(2 * i + 1, 1, chain)
-                block(2 * i + 2, 0, chain)
-
-            block(N_BLK - 1, 1, chain)
-            w1s = use(w1_copy, base + N_BLK - 1)
-            if chain:
-                accb[slot_m] += dot_nt(gbuf[1][...], w1buf[w1s])
-                rs_copy(accb, slot_m, rsb, m, sb_sem, rb_sem).start()
-
-        @pl.when(first)
-        def _():
-            blocks(False)
+            ws = use(flat_start, flat_wait, base + j)
+            u_load(m, j, slot).start()
+            if not start:
+                u_load(m, j - 1, 1 - slot).wait()
+            qbuf[slot][...] = dot_nt(xbuf[...], flat[ws]).astype(BF)
+            if not start:
+                slope(j - 1, 1 - slot)
+
+        block(0, 0)
+
+        @pl.loop(0, (N_BLK - 2) // 2)
+        def _(i):
+            block(2 * i + 1, 1)
+            block(2 * i + 2, 0)
+
+        block(N_BLK - 1, 1)
+        u_load(m, N_BLK - 1, 1).wait()
+        slope(N_BLK - 1, 1)
+        mid_copy(g_all, m).start()
 
         @pl.when(jnp.logical_not(first))
         def _():
-            blocks(True)
+            @pl.loop(0, DIM // HB)
+            def _(c):
+                ws = use(flat_start, flat_wait, base + N_BLK + 2 * c)
+                accb[slot_m, :, cols(c)] = dot_nt(mid[:, 0:DIM], flat[ws])
+                ws = use(flat_start, flat_wait, base + N_BLK + 2 * c + 1)
+                accb[slot_m, :, cols(c)] += dot_nt(mid[:, DIM:HID], flat[ws])
+                rs_part(accb, slot_m, rsb, m, c, sb_sem, rb_sem).start()
+
+        mid_copy(g_all, m).wait()
 
     def backward_post(m):
         slot = lax.rem(m, 2)
@@ -541,8 +573,8 @@
 
     lsum[...] = jnp.zeros((8, 128), F32)
     for j in range(W_SLOTS - 1):
-        w1_copy(j, j).start()
-        w2_copy(j, j).start()
+        tall_start(j)
+        flat_start(j)
 
     @pl.loop(0, N_MB + warm)
     def _(k):
@@ -563,7 +595,7 @@
 
         @pl.when(b_on)
         def _():
-            backward(b, b + jnp.minimum(k, N_MB))
+            backward(b)
             relay_back(b + LEAD3)
 
         @pl.when(jnp.logical_and(b_on, p_on))
@@ -580,7 +612,7 @@
 
         @pl.when(f_on)
         def _():
-            forward(k, k + jnp.maximum(b + 1, 0), lambda: pl.when(w_on)(weight_ops(v)[0]))
+            forward(k, lambda: pl.when(w_on)(weight_ops(v)[0]))
 
         @pl.when(jnp.logical_and(jnp.logical_not(b_on), p_on))
         def _():
@@ -590,34 +622,23 @@
         def _():
             relay(k - 2)
 
-        @pl.when(jnp.logical_and(pb_on, f_on))
+        @pl.when(pb_on)
         def _():
             backward_post(b)
 
-        half_tiles = DIM // WT // 2
-
         @pl.when(w_on)
         def _():
-            weight_ops(v)[1](0, half_tiles)
-
-        @pl.when(jnp.logical_and(pb_on, jnp.logical_not(f_on)))
-        def _():
-            backward_post(b)
-
-        @pl.when(w_on)
-        def _():
-            weight_ops(v)[1](half_tiles, 2 * half_tiles)
+            weight_ops(v)[1](0, DIM // WT)
 
     for half in range(2):
         pltpu.make_async_copy(lsum, lrx.at[half], lr_sem.at[half]).wait()
     loss[...] = lrx[0] + lrx[1]
 
     for j in range(W_SLOTS - 1):
-        w1_copy(j, (2 * N_MB * N_BLK + j) % W_SLOTS).wait()
-        w2_copy(j, (2 * N_MB * N_BLK + j) % W_SLOTS).wait()
+        tall_wait(j)
+        flat_wait(j)
     for m in (N_MB - 2, N_MB - 1):
         slot = m % 2
-        out_copy(gbuf, slot, g_all, m, 0, go_sem).wait()
         rs_copy(accf, slot, rsf, m, sf_sem, rf_sem).wait_send()
 
         @pl.when(jnp.logical_not(first))
@@ -672,8 +693,7 @@
             pltpu.VMEM((TOK, HB), BF), pltpu.VMEM((TOK, HB), BF),
             pltpu.VMEM((TOK, HB), BF), pltpu.VMEM((TOK, HB), BF),
             pltpu.VMEM((TOK, HB), BF), pltpu.VMEM((TOK, HB), BF),
-            pltpu.VMEM((TOK, HB), BF), pltpu.VMEM((TOK, HB), BF),
-            pltpu.VMEM((TOK, HB), BF),
+            pltpu.VMEM((TOK, HID), BF),
             pltpu.VMEM((2, TOK, DIM), F32),
             pltpu.VMEM((2, TOK, DIM), F32),
             pltpu.VMEM((HALF, DIM), F32),
@@ -686,7 +706,7 @@
             pltpu.VMEM((N_WT, WT, DIM), F32),
             pltpu.VMEM((8, 128), F32),
             pltpu.VMEM((2, 8, 128), F32),
-            dma((W_SLOTS, 2)), dma, dma((2,)), dma((2,)), dma((2,)), dma((2,)), dma((3,)), dma, dma((4,)), dma((N_WT,)), dma((N_WT,)),
+            dma((W_SLOTS,)), dma((W_SLOTS,)), dma, dma((2,)), dma, dma((2,)), dma((3,)), dma, dma((4,)), dma((N_WT,)), dma((N_WT,)),
             dma((N_MB, 2)), dma((N_MB, 2)), dma((N_MB,)), dma((N_MB,)), dma((2,)), dma((2,)), dma((2, 2)), dma((2, 2)),
             dma((N_MB,)), dma((2,)), dma((8,)), dma((2,)),
         ],

time: 2230 us -> 2260 us (1.013)
  Pallas kernels: 2220 us -> 2250 us
    pallas_call x1, Pallas kernels: 2140 us -> 2170 us  [run_pipeline(): pl.pallas_call(pipeline_kernel, out_shape=out_shape, in_specs=[hbm] * 4,...]
where the time goes in v6:
time: 2260 us; the launch traced here: 2250 us
  Pallas kernels  2250 us (100%)
    pallas_call x1, Pallas kernels, run_pipeline(): pl.pallas_call(pipeline_kernel, out_shape=out_shape, in_specs=[hbm] * 4,...  2170 us
    pallas_call x1, Pallas kernels, add_tail(): pl.pallas_call(tail_kernel, in_specs=[hbm] * 6, out_specs=[hbm] * 2, out_...  82.6 us

profile of v6, /device:TPU:0, one launch (start us, length us, event | category | flops | bytes accessed | tf_op | source)
XLA Modules:
  0.0 2254.5 jit_solution(3175073049959715672)
XLA Ops:
  0.6 2168.2 %pipeline.1 = (bf16[6144,2560]{1,0:T(8,128)(2,1)}, bf16[6144,2560]{1,0:T(8,128)(2,1)}, bf16[6144,5120]{1,0:T(8,128)(2,1)}, bf16[6144,5120]{1,0:T(8,128)(2,1)}, b...) custom-call(bf16[6144,2560]{1,0:T(8,128)(2,1)} %bitcast.7, ...), custom_call_target="tpu_custom_call" | custom-call | tf_op jit(solution)/shard_map/pipeline/pallas_call | solution.py:684
  2168.9 1.3 reduce_sum.9
  2170.8 82.6 %tail.1 = (f32[2560,5120]{1,0:T(8,128)}, f32[5120,2560]{1,0:T(8,128)}) custom-call(bf16[6144,2560]{1,0:T(8,128)(2,1)} %get-tuple-element.12.x_all, bf16[6144,2560]{1,0:T(8,128)(2,1)} %get-tuple-element.13.e_all, bf16[6144,5120]{1,0:T(8,128)(2,1)} %get-tuple-element.14.a_all, bf16[6144,5120]{1,0:T(8,128)(2,1)} %get-tuple-element.15.g_all, ...), custom_call_target="tpu_custom_call" | custom-call | tf_op jit(solution)/shard_map/tail/pallas_call | solution.py:809

commit v7 on v6

--- a/solution.py
+++ b/solution.py
@@ -15,15 +15,16 @@
 HID = 5120
 HB = 512
 N_BLK = HID // HB
-W_SLOTS = 3
+W_SLOTS = 4
 WT = HB // 2
 N_WT = 6
 GROUP = 4
 N_GRP = N_MB // GROUP - 1
 GTOK = GROUP * TOK
 N_ELEM = N_MB * TOK * DIM
-RELAY0 = 3
-RELAY3 = 6
+RELAY0 = 5
+RELAY3 = 8
+EAGER = 3
 LEAD3 = 3
 MESH = pl.DeviceIdType.MESH
 BF = jnp.bfloat16
@@ -397,14 +398,13 @@
                 yield (True if s < 3 else my != y), cp
 
     def backward(m):
-        slot_m = lax.rem(m, 2)
         base = m * n_back
         wait_in(e_all, m, er_sem)
         load_x(e_all, m)
 
-        @pl.when(jnp.logical_and(m >= 2, jnp.logical_not(first)))
-        def _():
-            rs_copy(accb, slot_m, rsb, m - 2, sb_sem, rb_sem).wait_send()
+        @pl.when(jnp.logical_and(m >= 1, jnp.logical_not(first)))
+        def _():
+            rs_copy(accb, 0, rsb, m - 1, sb_sem, rb_sem).wait_send()
 
         def slope(j, slot):
             mid[:, cols(j)] = (gelu_slope(uin[slot][...].astype(F32)) * qbuf[slot][...].astype(F32)).astype(BF)
@@ -436,10 +436,10 @@
             @pl.loop(0, DIM // HB)
             def _(c):
                 ws = use(flat_start, flat_wait, base + N_BLK + 2 * c)
-                accb[slot_m, :, cols(c)] = dot_nt(mid[:, 0:DIM], flat[ws])
+                accb[0, :, cols(c)] = dot_nt(mid[:, 0:DIM], flat[ws])
                 ws = use(flat_start, flat_wait, base + N_BLK + 2 * c + 1)
-                accb[slot_m, :, cols(c)] += dot_nt(mid[:, DIM:HID], flat[ws])
-                rs_part(accb, slot_m, rsb, m, c, sb_sem, rb_sem).start()
+                accb[0, :, cols(c)] += dot_nt(mid[:, DIM:HID], flat[ws])
+                rs_part(accb, 0, rsb, m, c, sb_sem, rb_sem).start()
 
         mid_copy(g_all, m).wait()
 
@@ -453,7 +453,7 @@
             for cp in yb_pair(m, slot):
                 cp.wait_send()
 
-        yb[slot] = (res[...].astype(F32) + (accb[slot, half_rows(my), :] + rsv[...])).astype(BF)
+        yb[slot] = (res[...].astype(F32) + (accb[0, half_rows(my), :] + rsv[...])).astype(BF)
         own, cross = yb_pair(m, slot)
         own.start()
         far = jnp.logical_and(last, m >= RELAY3)
@@ -583,7 +583,7 @@
         v = b - GROUP
         b_on = b >= 0
         f_on = k < N_MB
-        p_on = jnp.logical_and(p >= 0, p < N_MB)
+        p_on = jnp.logical_and(p >= EAGER, p < N_MB)
         pb_on = jnp.logical_and(b_on, jnp.logical_not(first))
         w_on = jnp.logical_and(v >= 0, jnp.logical_not(first))
 
@@ -614,6 +614,10 @@
         def _():
             forward(k, lambda: pl.when(w_on)(weight_ops(v)[0]))
 
+        @pl.when(k < EAGER)
+        def _():
+            forward_post(k)
+
         @pl.when(jnp.logical_and(jnp.logical_not(b_on), p_on))
         def _():
             forward_post(p)
@@ -622,13 +626,19 @@
         def _():
             relay(k - 2)
 
-        @pl.when(pb_on)
+        post_first = jnp.logical_or(f_on, b >= jnp.where(st == 1, N_MB - 1, N_MB - 2))
+
+        @pl.when(jnp.logical_and(pb_on, post_first))
         def _():
             backward_post(b)
 
         @pl.when(w_on)
         def _():
             weight_ops(v)[1](0, DIM // WT)
+
+        @pl.when(jnp.logical_and(pb_on, jnp.logical_not(post_first)))
+        def _():
+            backward_post(b)
 
     for half in range(2):
         pltpu.make_async_copy(lsum, lrx.at[half], lr_sem.at[half]).wait()
@@ -643,7 +653,8 @@
 
         @pl.when(jnp.logical_not(first))
         def _():
-            rs_copy(accb, slot, rsb, m, sb_sem, rb_sem).wait_send()
+            if m == N_MB - 1:
+                rs_copy(accb, 0, rsb, m, sb_sem, rb_sem).wait_send()
             for cp in yb_pair(m, slot):
                 cp.wait_send()
 
@@ -695,7 +706,7 @@
             pltpu.VMEM((TOK, HB), BF), pltpu.VMEM((TOK, HB), BF),
             pltpu.VMEM((TOK, HID), BF),
             pltpu.VMEM((2, TOK, DIM), F32),
-            pltpu.VMEM((2, TOK, DIM), F32),
+            pltpu.VMEM((1, TOK, DIM), F32),
             pltpu.VMEM((HALF, DIM), F32),
             pltpu.VMEM((HALF, DIM), BF),
             pltpu.VMEM((HALF, DIM), BF),
@@ -707,10 +718,10 @@
             pltpu.VMEM((8, 128), F32),
             pltpu.VMEM((2, 8, 128), F32),
             dma((W_SLOTS,)), dma((W_SLOTS,)), dma, dma((2,)), dma, dma((2,)), dma((3,)), dma, dma((4,)), dma((N_WT,)), dma((N_WT,)),
-            dma((N_MB, 2)), dma((N_MB, 2)), dma((N_MB,)), dma((N_MB,)), dma((2,)), dma((2,)), dma((2, 2)), dma((2, 2)),
+            dma((N_MB, 2)), dma((N_MB, 2)), dma((N_MB,)), dma((N_MB,)), dma((2,)), dma((1,)), dma((2, 2)), dma((2, 2)),
             dma((N_MB,)), dma((2,)), dma((8,)), dma((2,)),
         ],
-        compiler_params=pltpu.CompilerParams(vmem_limit_bytes=66_000_000, has_side_effects=True),
+        compiler_params=pltpu.CompilerParams(vmem_limit_bytes=67_000_000, has_side_effects=True),
         name="pipeline",
     )(x_in, tgt, w1, w2)
 

time: 2260 us -> 2200 us (0.973)
  Pallas kernels: 2250 us -> 2190 us
    pallas_call x1, Pallas kernels: 2170 us -> 2110 us  [run_pipeline(): pl.pallas_call(pipeline_kernel, out_shape=out_shape, in_specs=[hbm] * 4,...]
where the time goes in v7:
time: 2200 us
  Pallas kernels  2190 us (100%)
    pallas_call x1, Pallas kernels, run_pipeline(): pl.pallas_call(pipeline_kernel, out_shape=out_shape, in_specs=[hbm] * 4,...  2110 us
    pallas_call x1, Pallas kernels, add_tail(): pl.pallas_call(tail_kernel, in_specs=[hbm] * 6, out_specs=[hbm] * 2, out_...  82.6 us

profile of v7, /device:TPU:0, one launch (start us, length us, event | category | flops | bytes accessed | tf_op | source)
XLA Modules:
  0.0 2196.3 jit_solution(11575333169811970597)
XLA Ops:
  0.6 2110.0 %pipeline.1 = (bf16[6144,2560]{1,0:T(8,128)(2,1)}, bf16[6144,2560]{1,0:T(8,128)(2,1)}, bf16[6144,5120]{1,0:T(8,128)(2,1)}, bf16[6144,5120]{1,0:T(8,128)(2,1)}, b...) custom-call(bf16[6144,2560]{1,0:T(8,128)(2,1)} %bitcast.7, ...), custom_call_target="tpu_custom_call" | custom-call | tf_op jit(solution)/shard_map/pipeline/pallas_call | solution.py:695
  2110.7 1.3 reduce_sum.9
  2112.6 82.6 %tail.1 = (f32[2560,5120]{1,0:T(8,128)}, f32[5120,2560]{1,0:T(8,128)}) custom-call(bf16[6144,2560]{1,0:T(8,128)(2,1)} %get-tuple-element.12.x_all, bf16[6144,2560]{1,0:T(8,128)(2,1)} %get-tuple-element.13.e_all, bf16[6144,5120]{1,0:T(8,128)(2,1)} %get-tuple-element.14.a_all, bf16[6144,5120]{1,0:T(8,128)(2,1)} %get-tuple-element.15.g_all, ...), custom_call_target="tpu_custom_call" | custom-call | tf_op jit(solution)/shard_map/tail/pallas_call | solution.py:820
